TPU v7x, 32 devices: a whole 2x2x4 slice. The times are simulated.
32 devices in a mesh: rep: 1, r: 8 (over y, z), s: 4 (over x, core).
Axes of the slice: x: 2, y: 2, z: 4, core: 2. Of those that a mesh axis runs over, the one named last changes fastest.
Arguments:
- x: bfloat16 [32, 4096, 640], P(('rep', 'r', 's'))
- dy: bfloat16 [32, 4096, 640], P(('rep', 'r', 's'))
- w_gate: bfloat16 [2, 640, 2560], P(None, 's')
- w_up: bfloat16 [2, 640, 2560], P(None, 's')
- w_down: bfloat16 [2, 2560, 640], P(None, 's')
- m_w_gate: float32 [2, 640, 2560], P(None, 's')
- m_w_up: float32 [2, 640, 2560], P(None, 's')
- m_w_down: float32 [2, 2560, 640], P(None, 's')
- v_w_gate: float32 [2, 640, 2560], P(None, 's')
- v_w_up: float32 [2, 640, 2560], P(None, 's')
- v_w_down: float32 [2, 2560, 640], P(None, 's')
Outputs:
- output 1: bfloat16 [2, 640, 2560], P('rep', 's')
- output 2: bfloat16 [2, 640, 2560], P('rep', 's')
- output 3: bfloat16 [2, 2560, 640], P('rep', 's')
- output 4: float32 [2, 640, 2560], P('rep', 's')
- output 5: float32 [2, 640, 2560], P('rep', 's')
- output 6: float32 [2, 2560, 640], P('rep', 's')
- output 7: float32 [2, 640, 2560], P('rep', 's')
- output 8: float32 [2, 640, 2560], P('rep', 's')
- output 9: float32 [2, 2560, 640], P('rep', 's')
All inputs are finite; a program needn't handle non-finite values.
Results may differ from a plain program's by a relative error of at most 0.022.
Values are sent between devices in bfloat16 or wider.
A program may use at most 2 GiB of HBM per device.

v0:
```python
import jax
import jax.numpy as jnp
from jax import lax
from jax.sharding import PartitionSpec as P

NAMES = ("w_gate", "w_up", "w_down")


def matmul(a, w):
    return jnp.dot(a, w, preferred_element_type=jnp.float32).astype(jnp.bfloat16)


def normed(h):
    wide = h.astype(jnp.float32)
    scale = lax.rsqrt(jnp.mean(wide**2, -1, keepdims=True) + 1e-6)
    return (wide * scale).astype(jnp.bfloat16)


def layer(h, w):
    a = normed(h)
    gate = jnp.dot(a, w["w_gate"], preferred_element_type=jnp.float32)
    up = jnp.dot(a, w["w_up"], preferred_element_type=jnp.float32)
    return h + matmul((jax.nn.silu(gate) * up).astype(jnp.bfloat16), w["w_down"])


def adamw(w, m, v, g):
    m = 0.9 * m + 0.1 * g
    v = 0.95 * v + 0.05 * g * g
    step = m * lax.rsqrt(v + 1e-8) + 0.1 * w
    return (w - 0.02 * step).astype(jnp.bfloat16), m, v


def solution(mesh):
    def fetched(weights, number):
        return {name: lax.all_gather(w[number], "s", axis=0, tiled=True) for name, w in zip(NAMES, weights, strict=True)}

    def summed(term):
        return lax.psum(lax.psum_scatter(term, "s", scatter_dimension=0, tiled=True), "r")

    def step(x, dy, *arrays):
        weights, m, v = (arrays[i : i + 3] for i in (0, 3, 6))
        layers = weights[0].shape[0]
        h, kept = x[0], []
        for number in range(layers):
            kept.append(h)
            h = layer(h, fetched(weights, number))
        by_h, mine = dy[0], [None] * layers
        for number in reversed(range(layers)):
            _, back = jax.vjp(lambda w, h: layer(h, w), fetched(weights, number), kept[number])
            by_w, by_h = back(by_h)
            mine[number] = [summed(by_w[name]) for name in NAMES]
        gradients = [jnp.stack([mine[number][i] for number in range(layers)]).astype(jnp.float32) for i in range(3)]
        new = [adamw(w.astype(jnp.float32), m, v, g) for w, m, v, g in zip(weights, m, v, gradients, strict=True)]
        return tuple(one[which] for which in range(3) for one in new)

    states, cut = P(("rep", "r", "s"), None, None), P(None, "s", None)
    return jax.shard_map(
        step,
        mesh=mesh,
        in_specs=(states, states) + (cut,) * 9,
        out_specs=(P("rep", "s", None),) * 9,
        check_vma=False,
    )
```

profile of v0, /device:TPU:0, one launch (start us, length us, event | category | flops | bytes accessed | tf_op | source)
XLA Modules:
  0.0 792.3 jit_solution(12765440375145393698)
XLA Ops:
  7.2 2.8 fusion.87
  10.0 0.0 all-gather.15.cloned.1.call-start
  10.1 2.7 fusion.86
  12.8 0.0 all-gather.17.cloned.1.call-start
  12.8 1.3 fusion.85
  14.2 0.5 all-gather.21.cloned.1.call-update
  14.8 0.5 all-gather.23.cloned.1.call-update
  15.4 0.5 all-gather.19.cloned.1.call-update
  15.9 8.0 %copy.20 = bf16[1,4096,640]{1,2,0:T(8,128)(2,1)} copy(bf16[1,4096,640]{2,1,0:T(8,128)(2,1)} %param.11) | data formatting | bytes 10485760 | tf_op args[0]
  23.9 3.6 fusion.15
  27.6 8.0 %copy.21 = bf16[1,4096,640]{1,2,0:T(8,128)(2,1)} copy(bf16[1,4096,640]{2,1,0:T(8,128)(2,1)} %param.12) | data formatting | bytes 10485760 | tf_op args[1]
  35.5 6.4 all-gather.13.cloned.1.call-done
  41.9 26.5 %fusion.47 = f32[4096,2560]{1,0:T(8,128)} fusion(bf16[1,4096,640]{1,2,0:T(8,128)(2,1)} %copy.20, f32[4096]{0:T(1024)S(1)} %add_rsqrt_fusion, bf16[1,640,2560]{2,1,0:T(8,128)(2,1)} %all-gather.13.cloned.1.call-done), kind=kOutput, calls=%fused_computation.69 | convolution fusion | flops 13429637120 | bytes 50479104 | tf_op jit(solution)/shard_map/dot_general | solution.py:21
  68.5 4.6 all-gather.15.cloned.1.call-done
  73.1 41.4 %multiply_convert_fusion.1 = (bf16[4096,2560]{1,0:T(8,128)(2,1)}, f32[4096,2560]{1,0:T(8,128)}) fusion(f32[4096,2560]{1,0:T(8,128)} %fusion.47, bf16[1,640,2560]{2,1,0:T(8,128)(2,1)} %all-gather.15.cloned.1.call-done, bf16[1,4096,640]{1,2,0:T(8,128)(2,1)} %copy.20, f32[4096]{0:T(1024)S(1)} %add_rsqrt_fusion), kind=kOutput, calls=%fused_computation.17 | convolution fusion | flops 13492551680 | bytes 113393664 | tf_op jit(solution)/shard_map/dot_general | solution.py:22
  114.5 22.3 %fusion.19 = (f32[4096]{0:T(1024)S(1)}, bf16[4096,640]{0,1:T(8,128)(2,1)}) fusion(bf16[4096,2560]{1,0:T(8,128)(2,1)} %get-tuple-element.30, bf16[1,2560,640]{2,1,0:T(8,128)(2,1)} %all-gather.17.cloned.1.call-done, bf16[1,4096,640]{1,2,0:T(8,128)(2,1)} %copy.20), kind=kOutput, calls=%fused_computation.37 | convolution fusion | flops 13434875904 | bytes 34750464 | tf_op jit(solution)/shard_map/dot_general | solution.py:10
  136.8 0.6 copy-done.12
  137.4 22.5 %convolution_convert_fusion.1 = bf16[4096,2560]{1,0:T(8,128)(2,1)} fusion(bf16[1,4096,640]{2,1,0:T(8,128)(2,1)} %param.12, bf16[1,2560,640]{2,1,0:T(8,128)(2,1)} %all-gather.21.cloned.1.call-done), kind=kOutput, calls=%fused_computation.23 | convolution fusion | flops 13432258560 | bytes 29491200 | tf_op jit(solution)/shard_map/transpose(jvp())/dot_general | solution.py:10
  159.9 6.3 all-gather.23.cloned.1.call-done
  166.3 26.5 %fusion.39 = f32[4096,2560]{1,0:T(8,128)} fusion(bf16[4096,640]{0,1:T(8,128)(2,1)} %get-tuple-element.33, f32[4096]{0:T(1024)S(1)} %fusion.73, bf16[1,640,2560]{2,1,0:T(8,128)(2,1)} %all-gather.23.cloned.1.call-done), kind=kOutput, calls=%fused_computation.66 | convolution fusion | flops 13429637120 | bytes 50479104 | tf_op jit(solution)/shard_map/jvp()/dot_general | solution.py:22
  192.8 4.5 all-gather.19.cloned.1.call-done
  197.3 59.5 %fusion.2 = (bf16[4096,2560]{1,0:T(8,128)(2,1)}, f32[4096,2560]{1,0:T(8,128)}) fusion(f32[4096,2560]{1,0:T(8,128)} %fusion.39, bf16[4096,2560]{1,0:T(8,128)(2,1)} %convolution_convert_fusion.1, bf16[1,640,2560]{2,1,0:T(8,128)(2,1)} %all-gather.19.cloned.1.call-done, bf16[4096,640]{0,1:T(8,128)(2,1)} %get-tuple-element.33, f32[4096]{0:T(1024)S(1)} %fusion.73), kind=kOutput, calls=%fused_computation.8 | convolution fusion | flops 13555466240 | bytes 134365184 | tf_op jit(solution)/shard_map/jvp()/dot_general | solution.py:21
  256.8 20.6 %convolution_convert_fusion.2 = bf16[4096,640]{0,1:T(8,128)(2,1)} fusion(bf16[4096,2560]{1,0:T(8,128)(2,1)} %get-tuple-element.34, bf16[1,640,2560]{2,1,0:T(8,128)(2,1)} %all-gather.19.cloned.1.call-done), kind=kOutput, calls=%fused_computation.41 | convolution fusion | flops 13421772800 | bytes 29491200 | tf_op jit(solution)/shard_map/transpose(jvp())/dot_general | solution.py:21
  277.3 28.7 %fusion.21 = (f32[4096]{0:T(1024)S(1)}, bf16[4096,640]{0,1:T(8,128)(2,1)}) fusion(bf16[4096,640]{0,1:T(8,128)(2,1)} %get-tuple-element.33, bf16[4096,640]{0,1:T(8,128)(2,1)} %convolution_convert_fusion.2, bf16[1,640,2560]{2,1,0:T(8,128)(2,1)S(1)} %copy-done.17, bf16[4096,2560]{1,0:T(8,128)(2,1)} %convolution_convert_fusion.1, ...), kind=kOutput, calls=%fused_computation.39 | convolution fusion | flops 13500411904 | bytes 81936384 | tf_op jit(solution)/shard_map/transpose(jvp())/dot_general | solution.py:22
  306.1 11.8 %fusion.26 = bf16[4096,640]{0,1:T(8,128)(2,1)} fusion(bf16[4096,640]{0,1:T(8,128)(2,1)} %get-tuple-element.33, bf16[4096,640]{0,1:T(8,128)(2,1)} %get-tuple-element.37, bf16[1,4096,640]{1,2,0:T(8,128)(2,1)} %copy.21, f32[4096]{0:T(1024)S(1)} %multiply_multiply_fusion.3, f32[4096]{0:T(1024)S(1)} %fusion.73), kind=kLoop, calls=%fused_computation.45 | loop fusion | flops 18350080 | bytes 21004288 | tf_op jit(solution)/shard_map/transpose(jvp())/add_any | solution.py:14
  317.9 22.0 %convolution_convert_fusion.5 = bf16[2560,640]{1,0:T(8,128)(2,1)} fusion(bf16[4096,2560]{1,0:T(8,128)(2,1)} %get-tuple-element.30, bf16[4096,640]{0,1:T(8,128)(2,1)} %fusion.26), kind=kOutput, calls=%fused_computation.55 | convolution fusion | flops 13423411200 | bytes 29491200 | tf_op jit(solution)/shard_map/transpose(jvp())/dot_general | solution.py:10
  340.0 0.0 reduce-scatter.17.cloned.1.call-start
  340.0 33.5 %fusion.34 = bf16[2560,640]{1,0:T(8,128)(2,1)} fusion(bf16[1,4096,640]{2,1,0:T(8,128)(2,1)} %param.12, f32[4096,2560]{1,0:T(8,128)} %fusion.39, f32[4096,2560]{1,0:T(8,128)} %get-tuple-element.35), kind=kOutput, calls=%fused_computation.56 | convolution fusion | flops 13486325760 | bytes 92405760 | tf_op jit(solution)/shard_map/transpose(jvp())/dot_general | solution.py:10
  373.6 0.0 reduce-scatter.11.cloned.1.call-start
  373.6 22.1 %convolution_convert_fusion = bf16[4096,2560]{1,0:T(8,128)(2,1)} fusion(bf16[4096,640]{0,1:T(8,128)(2,1)} %fusion.26, bf16[1,2560,640]{2,1,0:T(8,128)(2,1)S(1)} %copy-done.16), kind=kOutput, calls=%fused_computation.22 | convolution fusion | flops 13432258560 | bytes 29491200 | tf_op jit(solution)/shard_map/transpose(jvp())/dot_general | solution.py:10
  395.8 29.0 %fusion.33 = bf16[640,2560]{1,0:T(8,128)(2,1)} fusion(bf16[4096,2560]{1,0:T(8,128)(2,1)} %convolution_convert_fusion, f32[4096,2560]{1,0:T(8,128)} %fusion.47, bf16[1,4096,640]{1,2,0:T(8,128)(2,1)} %copy.20, f32[4096]{0:T(1024)S(1)} %copy-done.15), kind=kOutput, calls=%fused_computation.53 | convolution fusion | flops 13494190080 | bytes 71450624 | tf_op jit(solution)/shard_map/transpose(jvp())/dot_general | solution.py:22
  424.8 0.0 reduce-scatter.13.cloned.1.call-start
  424.9 29.3 %fusion.29 = bf16[640,2560]{1,0:T(8,128)(2,1)} fusion(bf16[4096,2560]{1,0:T(8,128)(2,1)} %convolution_convert_fusion.1, bf16[4096,640]{0,1:T(8,128)(2,1)} %get-tuple-element.33, f32[4096]{0:T(1024)S(1)} %copy-done.11, f32[4096,2560]{1,0:T(8,128)} %get-tuple-element.35), kind=kOutput, calls=%fused_computation.51 | convolution fusion | flops 13494190080 | bytes 71450624 | tf_op jit(solution)/shard_map/transpose(jvp())/dot_general | solution.py:22
  454.2 0.0 reduce-scatter.7.cloned.1.call-start
  454.3 41.4 %fusion.30 = bf16[640,2560]{1,0:T(8,128)(2,1)} fusion(f32[4096,2560]{1,0:T(8,128)} %fusion.47, f32[4096,2560]{1,0:T(8,128)} %get-tuple-element.31, bf16[4096,2560]{1,0:T(8,128)(2,1)} %convolution_convert_fusion, bf16[1,4096,640]{1,2,0:T(8,128)(2,1)} %copy.20, f32[4096]{0:T(1024)S(1)} %copy-done.15), kind=kOutput, calls=%fused_computation.52 | convolution fusion | flops 13546618880 | bytes 113393664 | tf_op jit(solution)/shard_map/transpose(jvp())/dot_general | solution.py:21
  495.7 0.0 reduce-scatter.9.cloned.1.call-start
  495.8 20.8 %convolution_convert_fusion.4 = bf16[640,2560]{1,0:T(8,128)(2,1)} fusion(bf16[4096,2560]{1,0:T(8,128)(2,1)} %get-tuple-element.34, bf16[4096,640]{0,1:T(8,128)(2,1)} %get-tuple-element.33, f32[4096]{0:T(1024)S(1)} %copy-done.11), kind=kOutput, calls=%fused_computation.54 | convolution fusion | flops 13429637120 | bytes 29507584 | tf_op jit(solution)/shard_map/transpose(jvp())/dot_general | solution.py:21
  516.7 29.1 %reduce-scatter.7.cloned.1.call-done = bf16[160,2560]{1,0:T(8,128)(2,1)} async-done(((bf16[640,2560]{1,0:T(8,128)(2,1)}), bf16[160,2560]{1,0:T(8,128)(2,1)}) %reduce-scatter.7.cloned.1.call-update) | async-done | bytes 819216 | tf_op jit(solution)/shard_map/reduce_scatter | solution.py:38
  545.8 41.3 %reduce-scatter.9.cloned.1.call-done = bf16[160,2560]{1,0:T(8,128)(2,1)} async-done(((bf16[640,2560]{1,0:T(8,128)(2,1)}), bf16[160,2560]{1,0:T(8,128)(2,1)}) %reduce-scatter.9.cloned.1.call-update) | async-done | bytes 819216 | tf_op jit(solution)/shard_map/reduce_scatter | solution.py:38
  587.1 178.1 %all-reduce.3.cloned.1.call-done = (bf16[1,160,2560]{2,1,0:T(8,128)(2,1)}, bf16[1,160,2560]{2,1,0:T(8,128)(2,1)}, bf16[1,160,2560]{2,1,0:T(8,128)(2,1)}, bf16[1,...) async-done(((bf16[1,160,2560]{2,1,0:T(8,128)(2,1)}, bf16[1,160,2560]{2,1,0:T(8,128)(2,1)}, bf16[1,160,2560]{2,1,0:T(8,128)(2,1)}, ...) | async-done | bytes 4915216 | tf_op jit(solution)/shard_map/psum | solution.py:38
  765.3 7.3 fusion.59
  772.7 0.4 copy-done.4
  773.1 1.3 copy-done.5
  774.4 0.9 copy-done.6
  775.4 0.9 copy-done.7
  776.3 0.1 copy-done.8
  776.4 0.2 copy-done.9
  776.7 8.7 %fusion.51 = (bf16[2,160,2560]{2,1,0:T(8,128)(2,1)}, f32[2,160,2560]{2,1,0:T(8,128)}, f32[2,160,2560]{2,1,0:T(8,128)}, bf16[2,160,2560]{2,1,0:T(8,128)(2,1)}, f3...) fusion(bf16[2,160,2560]{2,1,0:T(8,128)(2,1)S(1)} %copy-done.2, bf16[1,160,2560]{2,1,0:T(8,128)(2,1)S(1)} %copy-done.8, ...), kind=kLoop, calls=%fused_computation.72 | loop fusion | flops 31129600 | bytes 36044800 | tf_op jit(solution)/shard_map/convert_element_type | solution.py:30
  (54 shorter events, 0.6 us)
Async XLA Ops:
  7.2 5.6 copy-start
  7.2 34.7 %all-gather.13.cloned.1.call-start = ((), (), s32[]{:S(2)}) async-start(), calls=%async_computation.12 | async-start | bytes 4096000 | tf_op jit(solution)/shard_map/all_gather | solution.py:35
  10.0 63.1 %all-gather.15.cloned.1.call-start = ((), (), s32[]{:S(2)}) async-start(), calls=%async_computation.13 | async-start | bytes 4096000 | tf_op jit(solution)/shard_map/all_gather | solution.py:35
  12.8 101.7 %all-gather.17.cloned.1.call-start = ((), (), s32[]{:S(2)}) async-start(), calls=%async_computation.14 | async-start | bytes 4096000 | tf_op jit(solution)/shard_map/all_gather | solution.py:35
  14.2 123.2 %all-gather.21.cloned.1.call-start = ((), (), s32[]{:S(2)}) async-start(), calls=%async_computation.16 | async-start | bytes 4096000 | tf_op jit(solution)/shard_map/all_gather | solution.py:35
  14.7 151.5 %all-gather.23.cloned.1.call-start = ((), (), s32[]{:S(2)}) async-start(), calls=%async_computation.17 | async-start | bytes 4096000 | tf_op jit(solution)/shard_map/all_gather | solution.py:35
  15.3 182.0 %all-gather.19.cloned.1.call-start = ((), (), s32[]{:S(2)}) async-start(), calls=%async_computation.15 | async-start | bytes 4096000 | tf_op jit(solution)/shard_map/all_gather | solution.py:35
  15.9 500.8 %reduce-scatter.15.cloned.1.call-start = ((), (), s32[]{:S(2)}) async-start(), calls=%async_computation.10 | async-start | bytes 4096000 | tf_op jit(solution)/shard_map/reduce_scatter | solution.py:38
  27.5 45.5 %copy-start.14 = (f32[4096]{0:T(1024)}, f32[4096]{0:T(1024)S(1)}, u32[]{:S(2)}) copy-start(f32[4096]{0:T(1024)S(1)} %add_rsqrt_fusion) | copy-start | bytes 49156
  136.8 0.6 copy-start.12
  137.4 168.7 %copy-start.10 = (f32[4096]{0:T(1024)}, f32[4096]{0:T(1024)S(1)}, u32[]{:S(2)}) copy-start(f32[4096]{0:T(1024)S(1)} %fusion.73) | copy-start | bytes 49156
  256.7 20.6 %copy-start.17 = (bf16[1,640,2560]{2,1,0:T(8,128)(2,1)S(1)}, bf16[1,640,2560]{2,1,0:T(8,128)(2,1)}, u32[]{:S(2)}) copy-start(bf16[1,640,2560]{2,1,0:T(8,128)(2,1)} %all-gather.23.cloned.1.call-done) | copy-start | bytes 9830404
  277.3 28.7 %copy-start.13 = (f32[4096]{0:T(1024)S(1)}, f32[4096]{0:T(1024)}, u32[]{:S(2)}) copy-start(f32[4096]{0:T(1024)} %copy-done.12) | copy-start | bytes 49156
  340.0 33.6 %copy-start.16 = (bf16[1,2560,640]{2,1,0:T(8,128)(2,1)S(1)}, bf16[1,2560,640]{2,1,0:T(8,128)(2,1)}, u32[]{:S(2)}) copy-start(bf16[1,2560,640]{2,1,0:T(8,128)(2,1)} %all-gather.17.cloned.1.call-done) | copy-start | bytes 9830404
  340.0 176.7 %reduce-scatter.17.cloned.1.call-start = ((), (), s32[]{:S(2)}) async-start(), calls=%async_computation.11 | async-start | bytes 4096000 | tf_op jit(solution)/shard_map/reduce_scatter | solution.py:38
  373.5 22.2 %copy-start.15 = (f32[4096]{0:T(1024)S(1)}, f32[4096]{0:T(1024)}, u32[]{:S(2)}) copy-start(f32[4096]{0:T(1024)} %copy-done.14) | copy-start | bytes 49156
  373.6 143.2 %reduce-scatter.11.cloned.1.call-start = ((), (), s32[]{:S(2)}) async-start(), calls=%async_computation.8 | async-start | bytes 4096000 | tf_op jit(solution)/shard_map/reduce_scatter | solution.py:38
  395.7 29.1 %copy-start.11 = (f32[4096]{0:T(1024)S(1)}, f32[4096]{0:T(1024)}, u32[]{:S(2)}) copy-start(f32[4096]{0:T(1024)} %copy-done.10) | copy-start | bytes 49156
  424.8 91.9 %reduce-scatter.13.cloned.1.call-start = ((), (), s32[]{:S(2)}) async-start(), calls=%async_computation.9 | async-start | bytes 4096000 | tf_op jit(solution)/shard_map/reduce_scatter | solution.py:38
  454.2 91.6 %reduce-scatter.7.cloned.1.call-start = ((), (), s32[]{:S(2)}) async-start(), calls=%async_computation.6 | async-start | bytes 4096000 | tf_op jit(solution)/shard_map/reduce_scatter | solution.py:38
  495.7 91.4 %reduce-scatter.9.cloned.1.call-start = ((), (), s32[]{:S(2)}) async-start(), calls=%async_computation.7 | async-start | bytes 4096000 | tf_op jit(solution)/shard_map/reduce_scatter | solution.py:38
  516.6 248.7 %copy-start.1 = (bf16[2,640,640]{2,1,0:T(8,128)(2,1)S(1)}, bf16[2,640,640]{2,1,0:T(8,128)(2,1)}, u32[]{:S(2)}) copy-start(bf16[2,640,640]{2,1,0:T(8,128)(2,1)} %param.15) | copy-start | bytes 4915204
  516.6 248.7 %all-reduce.3.cloned.1.call-start = ((), (), s32[]{:S(2)}) async-start(), calls=%async_computation.18 | async-start | bytes 9830400 | tf_op jit(solution)/shard_map/psum | solution.py:38
  765.2 7.4 copy-start.2
  765.3 7.4 copy-start.3
  765.3 7.8 copy-start.4
  765.3 9.2 %copy-start.5 = (f32[2,160,2560]{2,1,0:T(8,128)S(1)}, f32[2,160,2560]{2,1,0:T(8,128)}, u32[]{:S(2)}) copy-start(f32[2,160,2560]{2,1,0:T(8,128)} %param.16) | copy-start | bytes 9830404
  765.3 10.1 %copy-start.6 = (f32[2,160,2560]{2,1,0:T(8,128)S(1)}, f32[2,160,2560]{2,1,0:T(8,128)}, u32[]{:S(2)}) copy-start(f32[2,160,2560]{2,1,0:T(8,128)} %param.20) | copy-start | bytes 9830404
  765.3 11.0 %copy-start.7 = (f32[2,160,2560]{2,1,0:T(8,128)S(1)}, f32[2,160,2560]{2,1,0:T(8,128)}, u32[]{:S(2)}) copy-start(f32[2,160,2560]{2,1,0:T(8,128)} %param.17) | copy-start | bytes 9830404
  765.3 11.1 %copy-start.8 = (bf16[1,160,2560]{2,1,0:T(8,128)(2,1)S(1)}, bf16[1,160,2560]{2,1,0:T(8,128)(2,1)}, u32[]{:S(2)}) copy-start(bf16[1,160,2560]{2,1,0:T(8,128)(2,1)} %get-tuple-element.9) | copy-start | bytes 2457604
  765.3 11.4 %copy-start.9 = (bf16[1,160,2560]{2,1,0:T(8,128)(2,1)S(1)}, bf16[1,160,2560]{2,1,0:T(8,128)(2,1)}, u32[]{:S(2)}) copy-start(bf16[1,160,2560]{2,1,0:T(8,128)(2,1)} %get-tuple-element.10) | copy-start | bytes 2457604
Sparse Core Ops, SparseCore 0:
  10.2 31.7 all-gather.12
  44.1 28.9 all-gather.14
  75.2 28.9 all-gather.16
  106.2 28.9 all-gather.20
  137.2 28.9 all-gather.22
  168.3 28.9 all-gather.18
  340.1 38.2 reduce-scatter.14
  381.5 38.2 reduce-scatter.16
  424.9 38.2 reduce-scatter.10
  466.2 38.2 reduce-scatter.12
  507.6 38.2 reduce-scatter.6
  548.8 38.2 reduce-scatter.8
  591.5 173.7 all-reduce.2
where the time goes:
time: 801 us; the launch traced here: 792 us
  matrix products  446 us (56%)
  waiting for transfers between devices  272 us (34%)
  other arithmetic  31.5 us (4%)
  local copies, waits for them, and re-layouts  27.4 us (3%)
  between operations  14.5 us (2%)
    psum x1, waiting for transfers between devices, summed(): lax.psum(lax.psum_scatter(term, 's', scatter_dimension=0, tiled=True), 'r')  178 us
    dot_general x5, matrix products, layer(): gate = jnp.dot(a, w['w_gate'], preferred_element_type=jnp.float32)  169 us
    dot_general x5, matrix products, layer(): up = jnp.dot(a, w['w_up'], preferred_element_type=jnp.float32)  155 us
    dot_general x5, matrix products, matmul(): jnp.dot(a, w, preferred_element_type=jnp.float32).astype(jnp.bfloat16)  122 us
    reduce_scatter x6, waiting for transfers between devices, summed(): lax.psum_scatter(term, 's', scatter_dimension=0, tiled=True)  70.4 us
    all_gather x6, waiting for transfers between devices, fetched(): lax.all_gather(w[number], 's', axis=0, tiled=True)  21.9 us
    unnamed x38, local copies, waits for them, and re-layouts  20.6 us
  transfers between devices with their start and end apart: 13, of which 7 were waited for; matrix products, arithmetic and copies ran while one was open for 43% of the time, Pallas kernels for 0%

commit v1 on v0

v1 whole, which is shorter than its diff:
```python
import functools

import jax
import jax.numpy as jnp
from jax import lax
from jax.experimental import pallas as pl
from jax.experimental.pallas import tpu as pltpu
from jax.sharding import PartitionSpec as P

BF, F32 = jnp.bfloat16, jnp.float32
NN = (((1,), (0,)), ((), ()))
NT = (((1,), (1,)), ((), ()))
MESH = pl.DeviceIdType.MESH
ANY = pl.BlockSpec(memory_space=pl.ANY)
DMA = pltpu.SemaphoreType.DMA
VMEM_LIMIT = 67_000_000
CHUNKS, STEPS, TILE, SUB = 5, 4, 1024, 512


def dot(a, b, dims=NN):
    return lax.dot_general(a, b, dims, preferred_element_type=F32)


def normed(h):
    wide = h.astype(F32)
    return wide, lax.rsqrt(jnp.mean(wide * wide, -1, keepdims=True) + 1e-6)


def place():
    r, s = lax.axis_index("r"), lax.axis_index("s")
    x, core = s // 2, lax.rem(s, 2)
    return r, x, r // 4, core, lax.rem(r + 4, 8), lax.rem(s + 2, 4), s + 1 - 2 * core


def unpack(w_ref, wg, wu, wd):
    rows, width = w_ref.shape[2] // 3, w_ref.shape[3]
    part = width // 4
    for s in range(4):
        wg[s * rows : (s + 1) * rows, :] = w_ref[s // 2, s % 2, 0:rows, :]
        wu[s * rows : (s + 1) * rows, :] = w_ref[s // 2, s % 2, rows : 2 * rows, :]
        for k in range(4):
            wd[k * rows : (k + 1) * rows, s * part : (s + 1) * part] = w_ref[s // 2, s % 2, 2 * rows :, k * part : (k + 1) * part]


def pack(p_ref, dg, du, dd):
    rows, width = p_ref.shape[2] // 3, p_ref.shape[3]
    part = width // 4
    for s in range(4):
        p_ref[s // 2, s % 2, 0:rows, :] = dg[s * rows : (s + 1) * rows, :].astype(BF)
        p_ref[s // 2, s % 2, rows : 2 * rows, :] = du[s * rows : (s + 1) * rows, :].astype(BF)
        for k in range(4):
            p_ref[s // 2, s % 2, 2 * rows :, k * part : (k + 1) * part] = dd[k * rows : (k + 1) * rows, s * part : (s + 1) * part].astype(BF)


def remote(src, dst, send, recv, **to):
    return pltpu.make_async_remote_copy(src_ref=src, dst_ref=dst, send_sem=send, recv_sem=recv, device_id=to, device_id_type=MESH)


def forward_kernel(g_ref, u_ref, d_ref, x_ref, w_ref, h_ref, gate_ref, up_ref, a_s, out_s, wg, wu, wd, own, wbuf, keep, fetch, send, recv):
    j, t = pl.program_id(0), pl.program_id(1)
    step = j * STEPS + t
    _, x, y, core, other_y, other_x, other_core = place()
    count = 2 * CHUNKS
    half = own.shape[1] // 2
    mine, theirs = pl.ds(y * half, half), pl.ds((1 - y) * half, half)

    def over_core(k):
        return remote(own.at[k], w_ref.at[k, x, core], send.at[0, k], recv.at[0, k], s=other_core)

    def over_x(k):
        return remote(own.at[k, mine], w_ref.at[k, x, core, mine], send.at[1, k], recv.at[1, k], s=other_x)

    def over_y(k):
        at = w_ref.at[k, 1 - x, core, mine]
        return remote(at, at, send.at[2, k], recv.at[2, k], r=other_y)

    def on_first(k):
        at = w_ref.at[k, 1 - x, core, mine]
        return remote(at, at, send.at[3, k], recv.at[3, k], s=other_core)

    def on_second(k):
        at = w_ref.at[k, 1 - x, core, theirs]
        return remote(at, at, send.at[4, k], recv.at[4, k], s=other_core)

    def kept(k):
        return pltpu.make_async_copy(own.at[k], w_ref.at[k, x, core], keep.at[k])

    def fetched(k, slot):
        return pltpu.make_async_copy(w_ref.at[k], wbuf.at[slot], fetch.at[slot])

    def from_x(k):
        over_x(k).wait_recv()
        over_y(k).start()
        on_first(k).start()

    def from_y(k):
        over_y(k).wait_recv()
        on_second(k).start()

    def whole(k):
        for copy in (over_core, on_first, on_second):
            copy(k).wait_recv()
        kept(k).wait()

    @pl.when(step == 0)
    def _():
        barrier = pltpu.get_barrier_semaphore()
        for to in ({"s": other_core}, {"s": other_x}, {"r": other_y}):
            pl.semaphore_signal(barrier, inc=1, device_id=to, device_id_type=MESH)
        rows, part = own.shape[1] // 3, own.shape[2] // 4
        for layer in range(2):
            down = d_ref[layer].T
            for chunk in range(CHUNKS):
                k = layer * CHUNKS + chunk
                for q in range(4):
                    to = slice(q * part, (q + 1) * part)
                    at = slice((q * CHUNKS + chunk) * part, (q * CHUNKS + chunk + 1) * part)
                    own[k, 0:rows, to] = g_ref[layer, :, at]
                    own[k, rows : 2 * rows, to] = u_ref[layer, :, at]
                    own[k, 2 * rows :, to] = down[q * rows : (q + 1) * rows, chunk * part : (chunk + 1) * part]
        pl.semaphore_wait(barrier, 3)

        @pl.loop(0, count)
        def _(k):
            over_x(k).start()
            over_core(k).start()
            kept(k).start()

        from_x(0)
        from_x(1)
        from_y(0)
        whole(0)
        fetched(0, 0).start()

    @pl.when((lax.rem(step, 2) == 1) & (step < 2 * count - 4))
    def _():
        from_x((step + 3) // 2)

    @pl.when((lax.rem(step, 2) == 1) & (step < 2 * count - 2))
    def _():
        from_y((step + 1) // 2)

    @pl.when((lax.rem(step, 2) == 0) & (step > 0))
    def _():
        whole(step // 2)

    @pl.when(t == 0)
    def _():
        slot = lax.rem(j, 2)
        fetched(j, slot).wait()
        unpack(wbuf.at[slot], wg, wu, wd)

    @pl.when((t == STEPS - 1) & (j < CHUNKS - 1))
    def _():
        fetched(j + 1, lax.rem(j + 1, 2)).start()

    @pl.when(j == 0)
    def _():
        wide, scale = normed(x_ref[...])
        a_s[t] = (wide * scale).astype(BF)
        out_s[t] = jnp.zeros_like(out_s[t])

    for i in range(TILE // SUB):
        at = slice(i * SUB, (i + 1) * SUB)
        a = a_s[t, at, :]
        gate, up = dot(a, wg[...]), dot(a, wu[...])
        gate_ref[0, at, :] = gate
        up_ref[0, at, :] = up
        hidden = (gate * jax.nn.sigmoid(gate) * up).astype(BF)
        out_s[t, :, at] += dot(wd[...], hidden, NT)

    @pl.when(j == CHUNKS - 1)
    def _():
        h_ref[...] = x_ref[...] + out_s[t].astype(BF).T

    @pl.when(step == CHUNKS * STEPS - 1)
    def _():
        @pl.loop(0, count)
        def _(k):
            for copy in (over_core, over_x, over_y, on_first, on_second):
                copy(k).wait_send()


class Sum:
    def __init__(self, p_ref, g_ref, y_s, r1, r2, z_s, ry, rz, g_s, load, keep, send, recv):
        self.p, self.g, self.y_s, self.r1, self.r2, self.z_s, self.ry, self.rz, self.g_s = p_ref, g_ref, y_s, r1, r2, z_s, ry, rz, g_s
        self.load, self.keep, self.send, self.recv = load, keep, send, recv
        self.r, self.x, self.y, self.core, self.other_y, self.other_x, self.other_core = place()
        self.z = lax.rem(self.r, 4)

    @staticmethod
    def scratch(rows, width):
        piece = (rows // 2, width // 4)
        return [
            pltpu.VMEM((2, 2, rows, width), BF),
            pltpu.VMEM((CHUNKS, 2, rows, width), BF),
            pltpu.VMEM((CHUNKS, rows, width), BF),
            pltpu.VMEM((CHUNKS, 8) + piece, BF),
            pltpu.VMEM((CHUNKS, 4) + piece, BF),
            pltpu.VMEM((CHUNKS, 4) + piece, BF),
            pltpu.VMEM((CHUNKS, 8) + piece, BF),
            DMA((2,)),
            DMA((CHUNKS,)),
            DMA((CHUNKS, 10)),
            DMA((CHUNKS, 10)),
        ]

    def over_core(self, k):
        return remote(self.p.at[k, :, 1 - self.core], self.r1.at[k], self.send.at[k, 0], self.recv.at[k, 0], s=self.other_core)

    def loaded(self, k):
        return pltpu.make_async_copy(self.p.at[k, :, self.core], self.y_s.at[k % 2], self.load.at[k % 2])

    def over_x(self, k):
        return remote(self.y_s.at[k % 2, 1 - self.x], self.r2.at[k], self.send.at[k, 1], self.recv.at[k, 1], s=self.other_x)

    def over_y(self, k):
        return remote(self.z_s.at[k, pl.ds(4 * (1 - self.y), 4)], self.ry.at[k], self.send.at[k, 2], self.recv.at[k, 2], r=self.other_y)

    def over_z(self, k, d):
        to = lax.rem(self.z + d, 4)
        return remote(self.z_s.at[k, 4 * self.y + to], self.rz.at[k, self.z], self.send.at[k, 2 + d], self.recv.at[k, 2 + d], r=4 * self.y + to)

    def back_z(self, k, d):
        at = self.g_s.at[k, self.r]
        return remote(at, at, self.send.at[k, 5 + d], self.recv.at[k, 5 + d], r=4 * self.y + lax.rem(self.z + d, 4))

    def back_y(self, k):
        at = self.g_s.at[k, pl.ds(4 * self.y, 4)]
        return remote(at, at, self.send.at[k, 9], self.recv.at[k, 9], r=self.other_y)

    def kept(self, k):
        return pltpu.make_async_copy(self.g_s.at[k], self.g.at[k], self.keep.at[k])

    def greet(self):
        barrier = pltpu.get_barrier_semaphore()
        others = [{"r": 4 * self.y + lax.rem(self.z + d, 4)} for d in range(1, 4)]
        for to in [{"s": self.other_core}, {"s": self.other_x}, {"r": self.other_y}] + others:
            pl.semaphore_signal(barrier, inc=1, device_id=to, device_id_type=MESH)
        pl.semaphore_wait(barrier, 6)

    def start(self):
        for k in range(CHUNKS):
            self.over_core(k).start()
        for k in range(2):
            self.loaded(k).start()

    def add_core(self, k):
        self.loaded(k).wait()
        self.over_core(k).wait_recv()
        self.y_s[k % 2] = (self.y_s[k % 2].astype(F32) + self.r1[k].astype(F32)).astype(BF)
        self.over_x(k).start()

    def add_x(self, k):
        self.over_x(k).wait_recv()
        high, wide = self.z_s.shape[2:]
        for piece in range(8):
            at = (slice(piece // 4 * high, (piece // 4 + 1) * high), slice(piece % 4 * wide, (piece % 4 + 1) * wide))
            self.z_s[k, piece] = (self.y_s[(k % 2, self.x) + at].astype(F32) + self.r2[(k,) + at].astype(F32)).astype(BF)
        self.over_y(k).start()
        self.over_x(k).wait_send()
        if k + 2 < CHUNKS:
            self.loaded(k + 2).start()

    def add_y(self, k):
        self.over_y(k).wait_recv()
        mine = pl.ds(4 * self.y, 4)
        self.z_s[k, mine] = (self.z_s[k, mine].astype(F32) + self.ry[k].astype(F32)).astype(BF)
        for d in range(1, 4):
            self.over_z(k, d).start()

    def add_z(self, k):
        total = self.z_s[k, self.r].astype(F32)
        for d in range(1, 4):
            self.over_z(k, d).wait_recv()
        for d in range(1, 4):
            total += self.rz[k, lax.rem(self.z + d, 4)].astype(F32)
        self.g_s[k, self.r] = total.astype(BF)
        for d in range(1, 4):
            self.back_z(k, d).start()

    def gather_y(self, k):
        for d in range(1, 4):
            self.back_z(k, d).wait_recv()
        self.back_y(k).start()

    def finish(self, k):
        self.back_y(k).wait_recv()
        self.kept(k).start()

    def sent(self):
        for k in range(CHUNKS):
            self.kept(k).wait()
            self.over_core(k).wait_send()
            self.over_y(k).wait_send()
            self.back_y(k).wait_send()
            for d in range(1, 4):
                self.over_z(k, d).wait_send()
                self.back_z(k, d).wait_send()


def sum_kernel(p_ref, g_ref, *scratch):
    total = Sum(p_ref, g_ref, *scratch)
    total.greet()
    total.start()
    total.add_core(0)
    total.add_core(1)
    for n in range(CHUNKS + 4):
        if n < CHUNKS:
            total.add_x(n)
            if n + 2 < CHUNKS:
                total.add_core(n + 2)
        for late, stage in enumerate((total.add_y, total.add_z, total.gather_y, total.finish)):
            if 0 <= n - late < CHUNKS:
                stage(n - late)
    total.sent()


def backward_kernel(first, h_ref, dy_ref, w_ref, *refs):
    if first:
        gate_ref, up_ref, q_ref, p_ref, g_ref, at_s, dyt_s, dg_s, du_s, dd_s, wg, wu, wd, *scratch = refs
    else:
        p_ref, dh_ref, at_s, dyt_s, dg_s, du_s, dd_s, wg, wu, wd, a_s, da_s = refs
    j, t = pl.program_id(0), pl.program_id(1)

    if first:
        total = Sum(q_ref, g_ref, *scratch)
        stages = {0: [total.greet, total.start]}
        for k in range(CHUNKS):
            for stage, at in ((total.add_core, 1), (total.add_x, 4), (total.add_y, 6), (total.add_z, 8), (total.gather_y, 10), (total.finish, 12)):
                stages.setdefault(min(at + 3 * k, CHUNKS * STEPS - 1), []).append(functools.partial(stage, k))
        stages[CHUNKS * STEPS - 1].append(total.sent)
        for at, todo in sorted(stages.items()):

            @pl.when(j * STEPS + t == at)
            def _(todo=todo):
                for one in todo:
                    one()

    @pl.when(t == 0)
    def _():
        unpack(w_ref.at[0], wg, wu, wd)
        for s in (dg_s, du_s, dd_s):
            s[...] = jnp.zeros_like(s)

    @pl.when(j == 0)
    def _():
        wide, scale = normed(h_ref[...])
        a = (wide * scale).astype(BF)
        at_s[t] = a.T
        dyt_s[t] = dy_ref[...].T
        if not first:
            a_s[t] = a
            da_s[t] = jnp.zeros_like(da_s[t])

    for i in range(TILE // SUB):
        at = slice(i * SUB, (i + 1) * SUB)
        if first:
            gate, up = gate_ref[0, at, :], up_ref[0, at, :]
        else:
            a = a_s[t, at, :]
            gate, up = dot(a, wg[...]), dot(a, wu[...])
        by_hidden = dot(dy_ref[at, :], wd[...]).astype(BF).astype(F32)
        sig = jax.nn.sigmoid(gate)
        silu = gate * sig
        hidden = (silu * up).astype(BF)
        by_up = (by_hidden * silu).astype(BF)
        by_gate = (by_hidden * up * (sig + silu * (1.0 - sig))).astype(BF)
        dd_s[...] += dot(dyt_s[t, :, at], hidden)
        du_s[...] += dot(at_s[t, :, at], by_up)
        dg_s[...] += dot(at_s[t, :, at], by_gate)
        if not first:
            da_s[t, :, at] += dot(wg[...], by_gate, NT) + dot(wu[...], by_up, NT)

    @pl.when(t == STEPS - 1)
    def _():
        pack(p_ref.at[0], dg_s, du_s, dd_s)

    if not first:

        @pl.when(j == CHUNKS - 1)
        def _():
            wide, scale = normed(h_ref[...])
            da = da_s[t].astype(BF).T.astype(F32)
            inner = jnp.mean(da * wide, -1, keepdims=True)
            dh_ref[...] = dy_ref[...] + (da * scale - wide * (scale * scale * scale * inner)).astype(BF)


def adamw(w, m, v, g):
    g = g.astype(F32)
    m = 0.9 * m + 0.1 * g
    v = 0.95 * v + 0.05 * g * g
    step = m * lax.rsqrt(v + 1e-8) + 0.1 * w.astype(F32)
    return (w.astype(F32) - 0.02 * step).astype(BF), m, v


def columns_kernel(below, above, *refs):
    rows = refs[0].shape[1]
    part = below.shape[-1]

    def take(g):
        for chunk in range(CHUNKS):
            at = slice(chunk * part, (chunk + 1) * part)
            both = jnp.concatenate([g[chunk, 0, 0], g[chunk, 1, 0, : 2 * rows - g.shape[3]]], 0)
            for i in range(2):
                w, m, v = (refs[3 * i + k][0, :, at] for k in range(3))
                new = adamw(w, m, v, both[i * rows : (i + 1) * rows])
                for k in range(3):
                    refs[6 + 3 * i + k][0, :, at] = new[k]

    @pl.when(pl.program_id(0) == 0)
    def _():
        take(below)

    @pl.when(pl.program_id(0) == 1)
    def _():
        take(above)


def rows_kernel(below, above, w, m, v, *outs):
    def take(g):
        rows = w.shape[2] // 4
        skip = g.shape[3] - rows
        turned = jnp.concatenate([g[0, 0, q, skip:] for q in range(4)], 0).T
        for out, new in zip(outs, adamw(w[0], m[0], v[0], turned), strict=True):
            out[0] = new

    @pl.when(pl.program_id(0) == 0)
    def _():
        take(below)

    @pl.when(pl.program_id(0) == 1)
    def _():
        take(above)


def solution(mesh):
    def step(x, dy, *arrays):
        x, dy = x[0], dy[0]
        weights, m, v = (arrays[i : i + 3] for i in (0, 3, 6))
        tokens, d = x.shape
        layers, rows, ff = weights[0].shape
        width, deep = ff // CHUNKS, 3 * rows
        part = width // 4
        shape = jax.ShapeDtypeStruct

        def params(flops, **more):
            return dict(
                compiler_params=pltpu.CompilerParams(vmem_limit_bytes=VMEM_LIMIT, **more),
                cost_estimate=pl.CostEstimate(flops=flops * tokens * d * ff, bytes_accessed=0, transcendentals=0),
            )

        tok = pl.BlockSpec((TILE, d), lambda j, t: (t, 0))
        late = pl.BlockSpec((TILE, d), lambda j, t: (jnp.where(j == CHUNKS - 1, t, 0), 0))
        saved = pl.BlockSpec((1, TILE, width), lambda j, t: (j, t, 0))
        package = pl.BlockSpec((1, 2, 2, deep, width), lambda j, t: (j, 0, 0, 0, 0))
        above = pl.BlockSpec((1, 2, 2, deep, width), lambda j, t: (CHUNKS + j, 0, 0, 0, 0))
        packages = shape((CHUNKS, 2, 2, deep, width), BF)
        grads = shape((CHUNKS, 8, deep // 2, part), BF)
        matrices = [pltpu.VMEM((d, width), BF)] * 3
        across = [pltpu.VMEM((STEPS, d, TILE), BF)] * 2
        sums = [pltpu.VMEM((d, width), F32)] * 3
        count = layers * CHUNKS

        w, h, gate, up = pl.pallas_call(
            forward_kernel,
            grid=(CHUNKS, STEPS),
            in_specs=[pl.BlockSpec(w.shape, lambda j, t: (0, 0, 0), pipeline_mode=pl.Buffered(1)) for w in weights] + [tok],
            out_specs=[ANY, late, saved, saved],
            out_shape=[shape((count, 2, 2, deep, width), BF), shape(x.shape, BF)] + [shape((CHUNKS, tokens, width), F32)] * 2,
            scratch_shapes=[pltpu.VMEM((STEPS, TILE, d), BF), pltpu.VMEM((STEPS, d, TILE), F32)]
            + matrices
            + [pltpu.VMEM((count, deep, width), BF), pltpu.VMEM((2, 2, 2, deep, width), BF)]
            + [DMA((count,)), DMA((2,)), DMA((5, count)), DMA((5, count))],
            name="forward",
            **params(6, collective_id=0, has_side_effects=True),
        )(*weights, x)
        above_grads, dh = pl.pallas_call(
            functools.partial(backward_kernel, False),
            grid=(CHUNKS, STEPS),
            in_specs=[tok, tok, above],
            out_specs=[package, late],
            out_shape=[packages, shape(x.shape, BF)],
            scratch_shapes=across + sums + matrices + [pltpu.VMEM((STEPS, TILE, d), BF), pltpu.VMEM((STEPS, d, TILE), F32)],
            name="backward_1",
            **params(16),
        )(h, dy, w)
        below_grads, above_sum = pl.pallas_call(
            functools.partial(backward_kernel, True),
            grid=(CHUNKS, STEPS),
            in_specs=[tok, tok, package, saved, saved, ANY],
            out_specs=[package, ANY],
            out_shape=[packages, grads],
            scratch_shapes=across + sums + matrices + Sum.scratch(deep, width),
            name="backward_0",
            **params(8, collective_id=1, has_side_effects=True),
        )(x, dh, w, gate, up, above_grads)
        below_sum = pl.pallas_call(
            sum_kernel,
            in_specs=[ANY],
            out_specs=ANY,
            out_shape=grads,
            scratch_shapes=Sum.scratch(deep, width),
            name="last_sum",
            **params(1, collective_id=2, has_side_effects=True),
        )(below_grads)

        g = [total.reshape(CHUNKS, 2, 4, deep // 2, part) for total in (below_sum, above_sum)]
        block = pl.BlockSpec((1, rows, CHUNKS * part), lambda layer, s: (layer, 0, s))
        both = pl.BlockSpec((CHUNKS, 2, 1, deep // 2, part), lambda layer, s: (0, 0, s, 0, 0))
        new = pl.pallas_call(
            columns_kernel,
            grid=(layers, 4),
            in_specs=[both] * 2 + [block] * 6,
            out_specs=[block] * 6,
            out_shape=[shape((layers, rows, ff), t) for t in (BF, F32, F32)] * 2,
            name="columns",
            **params(1),
        )(*g, weights[0], m[0], v[0], weights[1], m[1], v[1])
        block = pl.BlockSpec((1, part, d), lambda layer, j: (layer, j, 0))
        both = pl.BlockSpec((1, 1, 4, deep // 2, part), lambda layer, j: (j, 1, 0, 0, 0))
        new += pl.pallas_call(
            rows_kernel,
            grid=(layers, CHUNKS),
            in_specs=[both] * 2 + [block] * 3,
            out_specs=[block] * 3,
            out_shape=[shape((layers, CHUNKS * part, d), t) for t in (BF, F32, F32)],
            name="rows",
            **params(1),
        )(*g, weights[2], m[2], v[2])
        return tuple(new[3 * i + k] for k in range(3) for i in range(3))

    states, cut = P(("rep", "r", "s"), None, None), P(None, "s", None)
    return jax.shard_map(step, mesh=mesh, in_specs=(states, states) + (cut,) * 9, out_specs=(P("rep", "s", None),) * 9, check_vma=False)
```

time: 801 us -> 485 us (0.61); the launches traced: 792 us -> 484 us
  Pallas kernels: 0 us -> 483 us
  matrix products: 446 us -> 0 us
  waiting for transfers between devices: 272 us -> 0 us
  other arithmetic: 31.5 us -> 0 us
  local copies, waits for them, and re-layouts: 27.4 us -> 0 us
  between operations: 14.5 us -> 0.84 us
    pallas_call x0 -> x6, Pallas kernels: none -> 483 us  [the longest x1 149 us: step(): pl.pallas_call(functools.partial(backward_kernel, False), grid=(CHUNKS, S...]
    dot_general x15 -> x0, matrix products: 446 us -> none  [the longest x5 169 us: layer(): gate = jnp.dot(a, w['w_gate'], preferred_element_type=jnp.float32)]
    psum x1 -> x0, waiting for transfers between devices: 178 us -> none  [summed(): lax.psum(lax.psum_scatter(term, 's', scatter_dimension=0, tiled=True), 'r')]
    reduce_scatter x6 -> x0, waiting for transfers between devices: 70.4 us -> none  [summed(): lax.psum_scatter(term, 's', scatter_dimension=0, tiled=True)]
    all_gather x6 -> x0, waiting for transfers between devices: 21.9 us -> none  [fetched(): lax.all_gather(w[number], 's', axis=0, tiled=True)]
    unnamed x38 -> x0, local copies, waits for them, and re-layouts: 20.6 us -> none
    convert_element_type x2 -> x0, other arithmetic: 16 us -> none  [adamw(): return ((w - 0.02 * step).astype(jnp.bfloat16), m, v)]
    add_any x1 -> x0, other arithmetic: 11.8 us -> none  [normed(): wide = h.astype(jnp.float32)]
  transfers between devices with their start and end apart: 13 -> 0, of which waited for: 7 -> 0; matrix products, arithmetic and copies ran while one was open for 43% -> 0% of each run, Pallas kernels for 0% -> 0%
where the time goes in v1:
time: 485 us; the launch traced here: 484 us
  Pallas kernels  483 us (100%)
    pallas_call x1, Pallas kernels, step(): pl.pallas_call(functools.partial(backward_kernel, False), grid=(CHUNKS, S...  149 us
    pallas_call x1, Pallas kernels, step(): pl.pallas_call(functools.partial(backward_kernel, True), grid=(CHUNKS, ST...  115 us
    pallas_call x1, Pallas kernels, step(): pl.pallas_call(sum_kernel, in_specs=[ANY], out_specs=ANY, out_shape=grads...  99.8 us
    pallas_call x1, Pallas kernels, step(): pl.pallas_call(forward_kernel, grid=(CHUNKS, STEPS), in_specs=[pl.BlockSp...  91.7 us
    pallas_call x1, Pallas kernels, step(): pl.pallas_call(columns_kernel, grid=(layers, 4), in_specs=[both] * 2 + [b...  16.4 us
    pallas_call x1, Pallas kernels, step(): pl.pallas_call(rows_kernel, grid=(layers, CHUNKS), in_specs=[both] * 2 +...  11.6 us

profile of v1, /device:TPU:0, one launch (start us, length us, event | category | flops | bytes accessed | tf_op | source)
XLA Modules:
  0.0 484.3 jit_solution(15628171840386217319)
XLA Ops:
  0.6 91.7 %forward.1 = (bf16[10,2,2,480,512]{4,3,2,1,0:T(8,128)(2,1)}, bf16[4096,640]{1,0:T(8,128)(2,1)}, f32[5,4096,512]{2,1,0:T(8,128)}, f32[5,4096,512]{2,1,0:T(8,128)}) custom-call(bf16[2,160,2560]{2,1,0:T(8,128)(2,1)} %refs_0_.1, bf16[2,160,2560]{2,1,0:T(8,128)(2,1)} %refs_3_.1, bf16[2,640,640]{2,1,0:T(8,128)(2,1)} %w.1, bf16[4096,640]{1,0:T(8,128)(2,1)} %bitcast.5), custom_call_target="tpu_custom_call" | custom-call | flops 40265318400 | tf_op jit(solution)/shard_map/forward/pallas_call | solution.py:465
  92.3 149.3 %backward_1.1 = (bf16[5,2,2,480,512]{4,3,2,1,0:T(8,128)(2,1)}, bf16[4096,640]{1,0:T(8,128)(2,1)}) custom-call(bf16[4096,640]{1,0:T(8,128)(2,1)} %get-tuple-element.26.h_ref, bf16[4096,640]{1,0:T(8,128)(2,1)} %bitcast.4, bf16[10,2,2,480,512]{4,3,2,1,0:T(8,128)(2,1)} %get-tuple-element.27.w_ref), custom_call_target="tpu_custom_call" | custom-call | flops 107374182400 | tf_op jit(solution)/shard_map/backward_1/pallas_call | solution.py:478
  241.7 114.7 %backward_0.1 = (bf16[5,2,2,480,512]{4,3,2,1,0:T(8,128)(2,1)}, bf16[5,8,240,128]{3,2,1,0:T(8,128)(2,1)}) custom-call(bf16[4096,640]{1,0:T(8,128)(2,1)} %bitcast.6, bf16[4096,640]{1,0:T(8,128)(2,1)} %get-tuple-element.28.dy_ref, bf16[10,2,2,480,512]{4,3,2,1,0:T(8,128)(2,1)} %get-tuple-element.27.w_ref, f32[5,4096,512]{2,1,0:T(8,128)} %get-tuple-element.29.refs_0_, ...), custom_call_target="tpu_custom_call" | custom-call | flops 53687091200 | tf_op jit(solution)/shard_map/backward_0/pallas_call | solution.py:488
  356.4 99.8 %last_sum.1 = bf16[5,8,240,128]{3,2,1,0:T(8,128)(2,1)} custom-call(bf16[5,2,2,480,512]{4,3,2,1,0:T(8,128)(2,1)} %get-tuple-element.32.p_ref), custom_call_target="tpu_custom_call" | custom-call | flops 6710886400 | tf_op jit(solution)/shard_map/last_sum/pallas_call | solution.py:498
  456.1 11.6 %rows.1 = (bf16[2,640,640]{2,1,0:T(8,128)(2,1)}, f32[2,640,640]{2,1,0:T(8,128)}, f32[2,640,640]{2,1,0:T(8,128)}) custom-call(bf16[5,2,4,240,128]{4,3,2,1,0:T(8,128)(2,1)} %bitcast.9, bf16[5,2,4,240,128]{4,3,2,1,0:T(8,128)(2,1)} %bitcast.7, bf16[2,640,640]{2,1,0:T(8,128)(2,1)} %w.1, f32[2,640,640]{2,1,0:T(8,128)} %m.1, f32[2,640,640]{2,1,0:T(8,128)} %v.1), custom_call_target="tpu_custom_call" | custom-call | flops 6710886400 | tf_op jit(solution)/shard_map/rows/pallas_call | solution.py:522
  467.7 16.4 %columns.1 = (bf16[2,160,2560]{2,1,0:T(8,128)(2,1)}, f32[2,160,2560]{2,1,0:T(8,128)}, f32[2,160,2560]{2,1,0:T(8,128)}, bf16[2,160,2560]{2,1,0:T(8,128)(2,1)}, f3...) custom-call(bf16[5,2,4,240,128]{4,3,2,1,0:T(8,128)(2,1)} %bitcast.10, bf16[5,2,4,240,128]{4,3,2,1,0:T(8,128)(2,1)} %bitcast.8, ...), custom_call_target="tpu_custom_call" | custom-call | flops 6710886400 | tf_op jit(solution)/shard_map/columns/pallas_call | solution.py:511

commit v2 on v1

--- a/solution.py
+++ b/solution.py
@@ -14,7 +14,7 @@
 ANY = pl.BlockSpec(memory_space=pl.ANY)
 DMA = pltpu.SemaphoreType.DMA
 VMEM_LIMIT = 67_000_000
-CHUNKS, STEPS, TILE, SUB = 5, 4, 1024, 512
+CHUNKS, STEPS, TILE, SUB, WIDE = 5, 4, 1024, 512, 1024
 
 
 def dot(a, b, dims=NN):
@@ -160,8 +160,8 @@
         a_s[t] = (wide * scale).astype(BF)
         out_s[t] = jnp.zeros_like(out_s[t])
 
-    for i in range(TILE // SUB):
-        at = slice(i * SUB, (i + 1) * SUB)
+    for i in range(TILE // WIDE):
+        at = slice(i * WIDE, (i + 1) * WIDE)
         a = a_s[t, at, :]
         gate, up = dot(a, wg[...]), dot(a, wu[...])
         gate_ref[0, at, :] = gate
@@ -182,100 +182,109 @@
 
 
 class Sum:
-    def __init__(self, p_ref, g_ref, y_s, r1, r2, z_s, ry, rz, g_s, load, keep, send, recv):
-        self.p, self.g, self.y_s, self.r1, self.r2, self.z_s, self.ry, self.rz, self.g_s = p_ref, g_ref, y_s, r1, r2, z_s, ry, rz, g_s
-        self.load, self.keep, self.send, self.recv = load, keep, send, recv
+    def __init__(self, count, g_ref, p_s, r1, r2, z_s, ry, rz, g_s, keep, send, recv, credit):
+        self.count, self.slots = count, p_s.shape[0]
+        self.g, self.p_s, self.r1, self.r2, self.z_s, self.ry, self.rz, self.g_s = g_ref, p_s, r1, r2, z_s, ry, rz, g_s
+        self.keep, self.send, self.recv, self.credit = keep, send, recv, credit
         self.r, self.x, self.y, self.core, self.other_y, self.other_x, self.other_core = place()
         self.z = lax.rem(self.r, 4)
+        self.partners = [({"s": self.other_core}, 0), ({"s": self.other_x}, 1), ({"r": self.other_y}, 2)]
+        self.partners += [({"r": self.along_z(d)}, 6 - d) for d in range(1, 4)]
 
     @staticmethod
-    def scratch(rows, width):
+    def scratch(slots, rows, width):
         piece = (rows // 2, width // 4)
         return [
-            pltpu.VMEM((2, 2, rows, width), BF),
-            pltpu.VMEM((CHUNKS, 2, rows, width), BF),
-            pltpu.VMEM((CHUNKS, rows, width), BF),
-            pltpu.VMEM((CHUNKS, 8) + piece, BF),
-            pltpu.VMEM((CHUNKS, 4) + piece, BF),
-            pltpu.VMEM((CHUNKS, 4) + piece, BF),
-            pltpu.VMEM((CHUNKS, 8) + piece, BF),
-            DMA((2,)),
-            DMA((CHUNKS,)),
-            DMA((CHUNKS, 10)),
-            DMA((CHUNKS, 10)),
+            pltpu.VMEM((slots, 2, 2, rows, width), BF),
+            pltpu.VMEM((slots, 2, rows, width), BF),
+            pltpu.VMEM((slots, rows, width), BF),
+            pltpu.VMEM((slots, 8) + piece, BF),
+            pltpu.VMEM((slots, 4) + piece, BF),
+            pltpu.VMEM((slots, 4) + piece, BF),
+            pltpu.VMEM((slots, 8) + piece, BF),
+            DMA((slots,)),
+            DMA((slots, 10)),
+            DMA((slots, 10)),
+            pltpu.SemaphoreType.REGULAR((6,)),
         ]
 
+    def along_z(self, d):
+        return 4 * self.y + lax.rem(self.z + d, 4)
+
+    def copy(self, src, dst, k, which, **to):
+        return remote(src, dst, self.send.at[k % self.slots, which], self.recv.at[k % self.slots, which], **to)
+
     def over_core(self, k):
-        return remote(self.p.at[k, :, 1 - self.core], self.r1.at[k], self.send.at[k, 0], self.recv.at[k, 0], s=self.other_core)
-
-    def loaded(self, k):
-        return pltpu.make_async_copy(self.p.at[k, :, self.core], self.y_s.at[k % 2], self.load.at[k % 2])
+        n = k % self.slots
+        return self.copy(self.p_s.at[n, :, 1 - self.core], self.r1.at[n], k, 0, s=self.other_core)
 
     def over_x(self, k):
-        return remote(self.y_s.at[k % 2, 1 - self.x], self.r2.at[k], self.send.at[k, 1], self.recv.at[k, 1], s=self.other_x)
+        n = k % self.slots
+        return self.copy(self.p_s.at[n, 1 - self.x, self.core], self.r2.at[n], k, 1, s=self.other_x)
 
     def over_y(self, k):
-        return remote(self.z_s.at[k, pl.ds(4 * (1 - self.y), 4)], self.ry.at[k], self.send.at[k, 2], self.recv.at[k, 2], r=self.other_y)
+        n = k % self.slots
+        return self.copy(self.z_s.at[n, pl.ds(4 * (1 - self.y), 4)], self.ry.at[n], k, 2, r=self.other_y)
 
     def over_z(self, k, d):
-        to = lax.rem(self.z + d, 4)
-        return remote(self.z_s.at[k, 4 * self.y + to], self.rz.at[k, self.z], self.send.at[k, 2 + d], self.recv.at[k, 2 + d], r=4 * self.y + to)
+        n = k % self.slots
+        return self.copy(self.z_s.at[n, self.along_z(d)], self.rz.at[n, self.z], k, 2 + d, r=self.along_z(d))
 
     def back_z(self, k, d):
-        at = self.g_s.at[k, self.r]
-        return remote(at, at, self.send.at[k, 5 + d], self.recv.at[k, 5 + d], r=4 * self.y + lax.rem(self.z + d, 4))
+        at = self.g_s.at[k % self.slots, self.r]
+        return self.copy(at, at, k, 5 + d, r=self.along_z(d))
 
     def back_y(self, k):
-        at = self.g_s.at[k, pl.ds(4 * self.y, 4)]
-        return remote(at, at, self.send.at[k, 9], self.recv.at[k, 9], r=self.other_y)
+        at = self.g_s.at[k % self.slots, pl.ds(4 * self.y, 4)]
+        return self.copy(at, at, k, 9, r=self.other_y)
 
     def kept(self, k):
-        return pltpu.make_async_copy(self.g_s.at[k], self.g.at[k], self.keep.at[k])
+        return pltpu.make_async_copy(self.g_s.at[k % self.slots], self.g.at[k], self.keep.at[k % self.slots])
 
     def greet(self):
         barrier = pltpu.get_barrier_semaphore()
-        others = [{"r": 4 * self.y + lax.rem(self.z + d, 4)} for d in range(1, 4)]
-        for to in [{"s": self.other_core}, {"s": self.other_x}, {"r": self.other_y}] + others:
+        for to, _ in self.partners:
             pl.semaphore_signal(barrier, inc=1, device_id=to, device_id_type=MESH)
         pl.semaphore_wait(barrier, 6)
 
-    def start(self):
-        for k in range(CHUNKS):
-            self.over_core(k).start()
-        for k in range(2):
-            self.loaded(k).start()
+    def begin(self, k):
+        if k >= self.slots:
+            for i in range(6):
+                pl.semaphore_wait(self.credit.at[i], 1)
+        self.over_core(k).start()
 
     def add_core(self, k):
-        self.loaded(k).wait()
+        n = k % self.slots
         self.over_core(k).wait_recv()
-        self.y_s[k % 2] = (self.y_s[k % 2].astype(F32) + self.r1[k].astype(F32)).astype(BF)
+        for x in range(2):
+            self.p_s[n, x, self.core] = (self.p_s[n, x, self.core].astype(F32) + self.r1[n, x].astype(F32)).astype(BF)
         self.over_x(k).start()
 
     def add_x(self, k):
+        n = k % self.slots
         self.over_x(k).wait_recv()
         high, wide = self.z_s.shape[2:]
         for piece in range(8):
             at = (slice(piece // 4 * high, (piece // 4 + 1) * high), slice(piece % 4 * wide, (piece % 4 + 1) * wide))
-            self.z_s[k, piece] = (self.y_s[(k % 2, self.x) + at].astype(F32) + self.r2[(k,) + at].astype(F32)).astype(BF)
+            self.z_s[n, piece] = (self.p_s[(n, self.x, self.core) + at].astype(F32) + self.r2[(n,) + at].astype(F32)).astype(BF)
         self.over_y(k).start()
-        self.over_x(k).wait_send()
-        if k + 2 < CHUNKS:
-            self.loaded(k + 2).start()
 
     def add_y(self, k):
+        n = k % self.slots
         self.over_y(k).wait_recv()
         mine = pl.ds(4 * self.y, 4)
-        self.z_s[k, mine] = (self.z_s[k, mine].astype(F32) + self.ry[k].astype(F32)).astype(BF)
+        self.z_s[n, mine] = (self.z_s[n, mine].astype(F32) + self.ry[n].astype(F32)).astype(BF)
         for d in range(1, 4):
             self.over_z(k, d).start()
 
     def add_z(self, k):
-        total = self.z_s[k, self.r].astype(F32)
+        n = k % self.slots
+        total = self.z_s[n, self.r].astype(F32)
         for d in range(1, 4):
             self.over_z(k, d).wait_recv()
         for d in range(1, 4):
-            total += self.rz[k, lax.rem(self.z + d, 4)].astype(F32)
-        self.g_s[k, self.r] = total.astype(BF)
+            total += self.rz[n, lax.rem(self.z + d, 4)].astype(F32)
+        self.g_s[n, self.r] = total.astype(BF)
         for d in range(1, 4):
             self.back_z(k, d).start()
 
@@ -287,55 +296,69 @@
     def finish(self, k):
         self.back_y(k).wait_recv()
         self.kept(k).start()
-
-    def sent(self):
-        for k in range(CHUNKS):
-            self.kept(k).wait()
-            self.over_core(k).wait_send()
-            self.over_y(k).wait_send()
-            self.back_y(k).wait_send()
-            for d in range(1, 4):
-                self.over_z(k, d).wait_send()
-                self.back_z(k, d).wait_send()
-
-
-def sum_kernel(p_ref, g_ref, *scratch):
-    total = Sum(p_ref, g_ref, *scratch)
-    total.greet()
-    total.start()
-    total.add_core(0)
-    total.add_core(1)
-    for n in range(CHUNKS + 4):
-        if n < CHUNKS:
-            total.add_x(n)
-            if n + 2 < CHUNKS:
-                total.add_core(n + 2)
-        for late, stage in enumerate((total.add_y, total.add_z, total.gather_y, total.finish)):
-            if 0 <= n - late < CHUNKS:
-                stage(n - late)
-    total.sent()
+        for copy in (self.over_core, self.over_x, self.over_y, self.back_y):
+            copy(k).wait_send()
+        for d in range(1, 4):
+            self.over_z(k, d).wait_send()
+            self.back_z(k, d).wait_send()
+
+    def release(self, k):
+        self.kept(k).wait()
+        if k + self.slots < self.count:
+            for to, i in self.partners:
+                pl.semaphore_signal(self.credit.at[i], inc=1, device_id=to, device_id_type=MESH)
+
+    def timed(self, begins, after):
+        stages = (self.begin, self.add_core, self.add_x, self.add_y, self.add_z, self.gather_y, self.finish, self.release)
+        return [(at + late, functools.partial(stage, k)) for k, at in enumerate(begins) for stage, late in zip(stages, (0,) + after, strict=True)]
+
+
+EARLY = 3
+
+
+def run_at(step, timed, last):
+    timed = sorted(timed, key=lambda one: one[0])
+    for at in sorted({one[0] for one in timed if one[0] <= last}):
+
+        @pl.when(step == at)
+        def _(at=at):
+            for when, what in timed:
+                if when == at:
+                    what()
+
+    return [what for when, what in timed if when > last]
 
 
 def backward_kernel(first, h_ref, dy_ref, w_ref, *refs):
     if first:
-        gate_ref, up_ref, q_ref, p_ref, g_ref, at_s, dyt_s, dg_s, du_s, dd_s, wg, wu, wd, *scratch = refs
+        gate_ref, up_ref, q_ref, g_ref, at_s, dyt_s, dg_s, du_s, dd_s, wg, wu, wd, *scratch, load = refs
+        total = Sum(2 * CHUNKS - EARLY, g_ref, *scratch)
     else:
-        p_ref, dh_ref, at_s, dyt_s, dg_s, du_s, dd_s, wg, wu, wd, a_s, da_s = refs
+        g_ref, q_ref, dh_ref, at_s, dyt_s, dg_s, du_s, dd_s, wg, wu, wd, a_s, da_s, *scratch, load = refs
+        total = Sum(EARLY, g_ref, *scratch)
     j, t = pl.program_id(0), pl.program_id(1)
+    step, last = j * STEPS + t, CHUNKS * STEPS - 1
+    p_s, slots = total.p_s, total.slots
 
     if first:
-        total = Sum(q_ref, g_ref, *scratch)
-        stages = {0: [total.greet, total.start]}
-        for k in range(CHUNKS):
-            for stage, at in ((total.add_core, 1), (total.add_x, 4), (total.add_y, 6), (total.add_z, 8), (total.gather_y, 10), (total.finish, 12)):
-                stages.setdefault(min(at + 3 * k, CHUNKS * STEPS - 1), []).append(functools.partial(stage, k))
-        stages[CHUNKS * STEPS - 1].append(total.sent)
-        for at, todo in sorted(stages.items()):
-
-            @pl.when(j * STEPS + t == at)
-            def _(todo=todo):
-                for one in todo:
-                    one()
+
+        def taken(i):
+            return pltpu.make_async_copy(q_ref.at[i], p_s.at[i], load.at[i])
+
+        timed = [(0, taken(i).start) for i in range(CHUNKS - EARLY)] + [(0, total.greet)]
+        timed += [(3 * i, taken(i).wait) for i in range(CHUNKS - EARLY)]
+        timed += total.timed((0, 3, 6, 9, 12, 16, last + 0.9), (1, 4, 6, 8, 10, 11, 12))
+        ahead = CHUNKS - EARLY
+    else:
+
+        def taken(i):
+            return pltpu.make_async_copy(p_s.at[(EARLY + i) % slots], q_ref.at[i], load.at[i])
+
+        timed = [(0, total.greet)] + total.timed((4, 8, 12), (1, 3, 4, 5, 6, 7, 7))
+        timed += [(STEPS * (EARLY + i + 1), taken(i).start) for i in range(CHUNKS - EARLY)]
+        timed += [(last + 2, taken(i).wait) for i in range(CHUNKS - EARLY)]
+        ahead = 0
+    rest = run_at(step, timed, last)
 
     @pl.when(t == 0)
     def _():
@@ -374,7 +397,7 @@
 
     @pl.when(t == STEPS - 1)
     def _():
-        pack(p_ref.at[0], dg_s, du_s, dd_s)
+        pack(p_s.at[lax.rem(j + ahead, slots)], dg_s, du_s, dd_s)
 
     if not first:
 
@@ -385,6 +408,11 @@
             inner = jnp.mean(da * wide, -1, keepdims=True)
             dh_ref[...] = dy_ref[...] + (da * scale - wide * (scale * scale * scale * inner)).astype(BF)
 
+    @pl.when(step == last)
+    def _():
+        for what in rest:
+            what()
+
 
 def adamw(w, m, v, g):
     g = g.astype(F32)
@@ -394,14 +422,14 @@
     return (w.astype(F32) - 0.02 * step).astype(BF), m, v
 
 
-def columns_kernel(below, above, *refs):
+def columns_kernel(early, late, *refs):
     rows = refs[0].shape[1]
-    part = below.shape[-1]
-
-    def take(g):
-        for chunk in range(CHUNKS):
+    part = early.shape[-1]
+
+    def take(chunks):
+        for chunk, (g, n) in enumerate(chunks):
             at = slice(chunk * part, (chunk + 1) * part)
-            both = jnp.concatenate([g[chunk, 0, 0], g[chunk, 1, 0, : 2 * rows - g.shape[3]]], 0)
+            both = jnp.concatenate([g[n, 0, 0], g[n, 1, 0, : 2 * rows - g.shape[3]]], 0)
             for i in range(2):
                 w, m, v = (refs[3 * i + k][0, :, at] for k in range(3))
                 new = adamw(w, m, v, both[i * rows : (i + 1) * rows])
@@ -410,14 +438,14 @@
 
     @pl.when(pl.program_id(0) == 0)
     def _():
-        take(below)
+        take([(late, CHUNKS - EARLY + n) for n in range(CHUNKS)])
 
     @pl.when(pl.program_id(0) == 1)
     def _():
-        take(above)
-
-
-def rows_kernel(below, above, w, m, v, *outs):
+        take([(early, n) for n in range(EARLY)] + [(late, n) for n in range(CHUNKS - EARLY)])
+
+
+def rows_kernel(early, late, w, m, v, *outs):
     def take(g):
         rows = w.shape[2] // 4
         skip = g.shape[3] - rows
@@ -425,13 +453,15 @@
         for out, new in zip(outs, adamw(w[0], m[0], v[0], turned), strict=True):
             out[0] = new
 
-    @pl.when(pl.program_id(0) == 0)
-    def _():
-        take(below)
-
-    @pl.when(pl.program_id(0) == 1)
-    def _():
-        take(above)
+    from_early = (pl.program_id(0) == 1) & (pl.program_id(1) < EARLY)
+
+    @pl.when(from_early)
+    def _():
+        take(early)
+
+    @pl.when(jnp.logical_not(from_early))
+    def _():
+        take(late)
 
 
 def solution(mesh):
@@ -455,8 +485,8 @@
         saved = pl.BlockSpec((1, TILE, width), lambda j, t: (j, t, 0))
         package = pl.BlockSpec((1, 2, 2, deep, width), lambda j, t: (j, 0, 0, 0, 0))
         above = pl.BlockSpec((1, 2, 2, deep, width), lambda j, t: (CHUNKS + j, 0, 0, 0, 0))
-        packages = shape((CHUNKS, 2, 2, deep, width), BF)
-        grads = shape((CHUNKS, 8, deep // 2, part), BF)
+        packages = shape((CHUNKS - EARLY, 2, 2, deep, width), BF)
+        grads = [shape((n, 8, deep // 2, part), BF) for n in (EARLY, 2 * CHUNKS - EARLY)]
         matrices = [pltpu.VMEM((d, width), BF)] * 3
         across = [pltpu.VMEM((STEPS, d, TILE), BF)] * 2
         sums = [pltpu.VMEM((d, width), F32)] * 3
@@ -475,54 +505,48 @@
             name="forward",
             **params(6, collective_id=0, has_side_effects=True),
         )(*weights, x)
-        above_grads, dh = pl.pallas_call(
+        early, waiting, dh = pl.pallas_call(
             functools.partial(backward_kernel, False),
             grid=(CHUNKS, STEPS),
             in_specs=[tok, tok, above],
-            out_specs=[package, late],
-            out_shape=[packages, shape(x.shape, BF)],
-            scratch_shapes=across + sums + matrices + [pltpu.VMEM((STEPS, TILE, d), BF), pltpu.VMEM((STEPS, d, TILE), F32)],
+            out_specs=[ANY, ANY, late],
+            out_shape=[grads[0], packages, shape(x.shape, BF)],
+            scratch_shapes=across + sums + matrices + [pltpu.VMEM((STEPS, TILE, d), BF), pltpu.VMEM((STEPS, d, TILE), F32)] + Sum.scratch(2, deep, width) + [DMA((2,))],
             name="backward_1",
-            **params(16),
+            **params(16, collective_id=1, has_side_effects=True),
         )(h, dy, w)
-        below_grads, above_sum = pl.pallas_call(
+        rest = pl.pallas_call(
             functools.partial(backward_kernel, True),
             grid=(CHUNKS, STEPS),
             in_specs=[tok, tok, package, saved, saved, ANY],
-            out_specs=[package, ANY],
-            out_shape=[packages, grads],
-            scratch_shapes=across + sums + matrices + Sum.scratch(deep, width),
+            out_specs=ANY,
+            out_shape=grads[1],
+            scratch_shapes=across + sums + matrices + Sum.scratch(4, deep, width) + [DMA((2,))],
             name="backward_0",
-            **params(8, collective_id=1, has_side_effects=True),
-        )(x, dh, w, gate, up, above_grads)
-        below_sum = pl.pallas_call(
-            sum_kernel,
-            in_specs=[ANY],
-            out_specs=ANY,
-            out_shape=grads,
-            scratch_shapes=Sum.scratch(deep, width),
-            name="last_sum",
-            **params(1, collective_id=2, has_side_effects=True),
-        )(below_grads)
-
-        g = [total.reshape(CHUNKS, 2, 4, deep // 2, part) for total in (below_sum, above_sum)]
+            **params(8, collective_id=2, has_side_effects=True),
+        )(x, dh, w, gate, up, waiting)
+
+        g = [total.reshape(-1, 2, 4, deep // 2, part) for total in (early, rest)]
         block = pl.BlockSpec((1, rows, CHUNKS * part), lambda layer, s: (layer, 0, s))
-        both = pl.BlockSpec((CHUNKS, 2, 1, deep // 2, part), lambda layer, s: (0, 0, s, 0, 0))
+        both = [pl.BlockSpec((total.shape[0], 2, 1, deep // 2, part), lambda layer, s: (0, 0, s, 0, 0)) for total in g]
         new = pl.pallas_call(
             columns_kernel,
             grid=(layers, 4),
-            in_specs=[both] * 2 + [block] * 6,
+            in_specs=both + [block] * 6,
             out_specs=[block] * 6,
             out_shape=[shape((layers, rows, ff), t) for t in (BF, F32, F32)] * 2,
             name="columns",
             **params(1),
         )(*g, weights[0], m[0], v[0], weights[1], m[1], v[1])
         block = pl.BlockSpec((1, part, d), lambda layer, j: (layer, j, 0))
-        both = pl.BlockSpec((1, 1, 4, deep // 2, part), lambda layer, j: (j, 1, 0, 0, 0))
+        both = [
+            pl.BlockSpec((1, 1, 4, deep // 2, part), lambda layer, j: (jnp.minimum(j, EARLY - 1), 1, 0, 0, 0)),
+            pl.BlockSpec((1, 1, 4, deep // 2, part), lambda layer, j: (jnp.where(layer == 0, j + CHUNKS - EARLY, jnp.maximum(j - EARLY, 0)), 1, 0, 0, 0)),
+        ]
         new += pl.pallas_call(
             rows_kernel,
             grid=(layers, CHUNKS),
-            in_specs=[both] * 2 + [block] * 3,
+            in_specs=both + [block] * 3,
             out_specs=[block] * 3,
             out_shape=[shape((layers, CHUNKS * part, d), t) for t in (BF, F32, F32)],
             name="rows",

time: 485 us -> 427 us (0.88)
  Pallas kernels: 483 us -> 425 us
    pallas_call x3 -> x2, Pallas kernels: 128 us -> 27.6 us  [the longest x1 16.4 us: step(): pl.pallas_call(columns_kernel, grid=(layers, 4), in_specs=both + [block]...]
    pallas_call x1, Pallas kernels: 115 us -> 146 us  [step(): pl.pallas_call(functools.partial(backward_kernel, True), grid=(CHUNKS, ST...]
    pallas_call x1, Pallas kernels: 149 us -> 162 us  [step(): pl.pallas_call(functools.partial(backward_kernel, False), grid=(CHUNKS, S...]
where the time goes in v2:
time: 427 us; the launch traced here: 426 us
  Pallas kernels  425 us (100%)
    pallas_call x1, Pallas kernels, step(): pl.pallas_call(functools.partial(backward_kernel, False), grid=(CHUNKS, S...  162 us
    pallas_call x1, Pallas kernels, step(): pl.pallas_call(functools.partial(backward_kernel, True), grid=(CHUNKS, ST...  146 us
    pallas_call x1, Pallas kernels, step(): pl.pallas_call(forward_kernel, grid=(CHUNKS, STEPS), in_specs=[pl.BlockSp...  90 us
    pallas_call x1, Pallas kernels, step(): pl.pallas_call(columns_kernel, grid=(layers, 4), in_specs=both + [block]...  16.4 us
    pallas_call x1, Pallas kernels, step(): pl.pallas_call(rows_kernel, grid=(layers, CHUNKS), in_specs=both + [block...  11.2 us

profile of v2, /device:TPU:0, one launch (start us, length us, event | category | flops | bytes accessed | tf_op | source)
XLA Modules:
  0.0 426.3 jit_solution(2038454752888971651)
XLA Ops:
  0.6 90.0 %forward.1 = (bf16[10,2,2,480,512]{4,3,2,1,0:T(8,128)(2,1)}, bf16[4096,640]{1,0:T(8,128)(2,1)}, f32[5,4096,512]{2,1,0:T(8,128)}, f32[5,4096,512]{2,1,0:T(8,128)}) custom-call(bf16[2,160,2560]{2,1,0:T(8,128)(2,1)} %refs_0_.1, bf16[2,160,2560]{2,1,0:T(8,128)(2,1)} %refs_3_.1, bf16[2,640,640]{2,1,0:T(8,128)(2,1)} %w.1, bf16[4096,640]{1,0:T(8,128)(2,1)} %bitcast.5), custom_call_target="tpu_custom_call" | custom-call | flops 40265318400 | tf_op jit(solution)/shard_map/forward/pallas_call | solution.py:495
  90.6 161.6 %backward_1.1 = (bf16[3,8,240,128]{3,2,1,0:T(8,128)(2,1)}, bf16[2,2,2,480,512]{4,3,2,1,0:T(8,128)(2,1)}, bf16[4096,640]{1,0:T(8,128)(2,1)}) custom-call(bf16[4096,640]{1,0:T(8,128)(2,1)} %get-tuple-element.25.h_ref, bf16[4096,640]{1,0:T(8,128)(2,1)} %bitcast.4, bf16[10,2,2,480,512]{4,3,2,1,0:T(8,128)(2,1)} %get-tuple-element.26.w_ref), custom_call_target="tpu_custom_call" | custom-call | flops 107374182400 | tf_op jit(solution)/shard_map/backward_1/pallas_call | solution.py:508
  252.2 146.3 %backward_0.1 = bf16[7,8,240,128]{3,2,1,0:T(8,128)(2,1)} custom-call(bf16[4096,640]{1,0:T(8,128)(2,1)} %bitcast.6, bf16[4096,640]{1,0:T(8,128)(2,1)} %get-tuple-element.28.dy_ref, bf16[10,2,2,480,512]{4,3,2,1,0:T(8,128)(2,1)} %get-tuple-element.26.w_ref, f32[5,4096,512]{2,1,0:T(8,128)} %get-tuple-element.29.refs_0_, ...), custom_call_target="tpu_custom_call" | custom-call | flops 53687091200 | tf_op jit(solution)/shard_map/backward_0/pallas_call | solution.py:518
  398.5 11.2 %rows.1 = (bf16[2,640,640]{2,1,0:T(8,128)(2,1)}, f32[2,640,640]{2,1,0:T(8,128)}, f32[2,640,640]{2,1,0:T(8,128)}) custom-call(bf16[3,2,4,240,128]{4,3,2,1,0:T(8,128)(2,1)} %bitcast.9, bf16[7,2,4,240,128]{4,3,2,1,0:T(8,128)(2,1)} %bitcast.7, bf16[2,640,640]{2,1,0:T(8,128)(2,1)} %w.1, f32[2,640,640]{2,1,0:T(8,128)} %m.1, f32[2,640,640]{2,1,0:T(8,128)} %v.1), custom_call_target="tpu_custom_call" | custom-call | flops 6710886400 | tf_op jit(solution)/shard_map/rows/pallas_call | solution.py:546
  409.7 16.4 %columns.1 = (bf16[2,160,2560]{2,1,0:T(8,128)(2,1)}, f32[2,160,2560]{2,1,0:T(8,128)}, f32[2,160,2560]{2,1,0:T(8,128)}, bf16[2,160,2560]{2,1,0:T(8,128)(2,1)}, f3...) custom-call(bf16[3,2,4,240,128]{4,3,2,1,0:T(8,128)(2,1)} %bitcast.10, bf16[7,2,4,240,128]{4,3,2,1,0:T(8,128)(2,1)} %bitcast.8, ...), custom_call_target="tpu_custom_call" | custom-call | flops 6710886400 | tf_op jit(solution)/shard_map/columns/pallas_call | solution.py:532

commit v3 on v2

--- a/solution.py
+++ b/solution.py
@@ -203,8 +203,8 @@
             pltpu.VMEM((slots, 4) + piece, BF),
             pltpu.VMEM((slots, 8) + piece, BF),
             DMA((slots,)),
-            DMA((slots, 10)),
-            DMA((slots, 10)),
+            DMA((slots, 17)),
+            DMA((slots, 17)),
             pltpu.SemaphoreType.REGULAR((6,)),
         ]
 
@@ -218,25 +218,36 @@
         n = k % self.slots
         return self.copy(self.p_s.at[n, :, 1 - self.core], self.r1.at[n], k, 0, s=self.other_core)
 
-    def over_x(self, k):
+    def over_x(self, k, h):
         n = k % self.slots
-        return self.copy(self.p_s.at[n, 1 - self.x, self.core], self.r2.at[n], k, 1, s=self.other_x)
-
-    def over_y(self, k):
-        n = k % self.slots
-        return self.copy(self.z_s.at[n, pl.ds(4 * (1 - self.y), 4)], self.ry.at[n], k, 2, r=self.other_y)
+        rows = self.rows(self.y if h else 1 - self.y)
+        return self.copy(self.p_s.at[n, 1 - self.x, self.core, rows], self.r2.at[n, rows], k, 1 + h, s=self.other_x)
+
+    def over_y(self, k, d):
+        n, at = k % self.slots, lax.rem(self.z + d, 4)
+        return self.copy(self.z_s.at[n, 4 * (1 - self.y) + at], self.ry.at[n, at], k, 3 + d, r=self.other_y)
 
     def over_z(self, k, d):
         n = k % self.slots
-        return self.copy(self.z_s.at[n, self.along_z(d)], self.rz.at[n, self.z], k, 2 + d, r=self.along_z(d))
+        return self.copy(self.z_s.at[n, self.along_z(d)], self.rz.at[n, self.z], k, 6 + d, r=self.along_z(d))
 
     def back_z(self, k, d):
         at = self.g_s.at[k % self.slots, self.r]
-        return self.copy(at, at, k, 5 + d, r=self.along_z(d))
-
-    def back_y(self, k):
-        at = self.g_s.at[k % self.slots, pl.ds(4 * self.y, 4)]
-        return self.copy(at, at, k, 9, r=self.other_y)
+        return self.copy(at, at, k, 9 + d, r=self.along_z(d))
+
+    def back_y(self, k, d):
+        at = self.g_s.at[k % self.slots, self.along_z(d)]
+        return self.copy(at, at, k, 13 + d, r=self.other_y)
+
+    def rows(self, y):
+        high = self.z_s.shape[2]
+        return pl.ds(pl.multiple_of(y * high, high), high)
+
+    def held(self, k, y, d):
+        n, wide = k % self.slots, self.z_s.shape[3]
+        at = (self.rows(y), pl.ds(pl.multiple_of(lax.rem(self.z + d, 4) * wide, wide), wide))
+        parts = self.p_s[(n, self.x, self.core) + at], self.r1[(n, self.x) + at], self.r2[(n,) + at]
+        return parts[0].astype(F32) + parts[1].astype(F32) + parts[2].astype(F32)
 
     def kept(self, k):
         return pltpu.make_async_copy(self.g_s.at[k % self.slots], self.g.at[k], self.keep.at[k % self.slots])
@@ -254,32 +265,33 @@
         self.over_core(k).start()
 
     def add_core(self, k):
-        n = k % self.slots
+        n, away = k % self.slots, 1 - self.x
         self.over_core(k).wait_recv()
-        for x in range(2):
-            self.p_s[n, x, self.core] = (self.p_s[n, x, self.core].astype(F32) + self.r1[n, x].astype(F32)).astype(BF)
-        self.over_x(k).start()
+        for h in range(2):
+            rows = self.rows(self.y if h else 1 - self.y)
+            both = self.p_s[n, away, self.core, rows].astype(F32) + self.r1[n, away, rows].astype(F32)
+            self.p_s[n, away, self.core, rows] = both.astype(BF)
+            self.over_x(k, h).start()
 
     def add_x(self, k):
-        n = k % self.slots
-        self.over_x(k).wait_recv()
-        high, wide = self.z_s.shape[2:]
-        for piece in range(8):
-            at = (slice(piece // 4 * high, (piece // 4 + 1) * high), slice(piece % 4 * wide, (piece % 4 + 1) * wide))
-            self.z_s[n, piece] = (self.p_s[(n, self.x, self.core) + at].astype(F32) + self.r2[(n,) + at].astype(F32)).astype(BF)
-        self.over_y(k).start()
+        n, away = k % self.slots, 1 - self.y
+        self.over_x(k, 0).wait_recv()
+        for d in (1, 2, 3, 0):
+            self.z_s[n, 4 * away + lax.rem(self.z + d, 4)] = self.held(k, away, d).astype(BF)
+            self.over_y(k, d).start()
 
     def add_y(self, k):
         n = k % self.slots
-        self.over_y(k).wait_recv()
-        mine = pl.ds(4 * self.y, 4)
-        self.z_s[n, mine] = (self.z_s[n, mine].astype(F32) + self.ry[n].astype(F32)).astype(BF)
-        for d in range(1, 4):
+        self.over_x(k, 1).wait_recv()
+        for d in (1, 2, 3):
+            self.over_y(k, d).wait_recv()
+            self.z_s[n, self.along_z(d)] = (self.held(k, self.y, d) + self.ry[n, lax.rem(self.z + d, 4)].astype(F32)).astype(BF)
             self.over_z(k, d).start()
 
     def add_z(self, k):
         n = k % self.slots
-        total = self.z_s[n, self.r].astype(F32)
+        self.over_y(k, 0).wait_recv()
+        total = self.held(k, self.y, 0) + self.ry[n, self.z].astype(F32)
         for d in range(1, 4):
             self.over_z(k, d).wait_recv()
         for d in range(1, 4):
@@ -287,17 +299,23 @@
         self.g_s[n, self.r] = total.astype(BF)
         for d in range(1, 4):
             self.back_z(k, d).start()
+        self.back_y(k, 0).start()
 
     def gather_y(self, k):
-        for d in range(1, 4):
-            self.back_z(k, d).wait_recv()
-        self.back_y(k).start()
+        for d in (1, 3, 2):
+            self.back_z(k, 4 - d).wait_recv()
+            self.back_y(k, d).start()
 
     def finish(self, k):
-        self.back_y(k).wait_recv()
+        for d in range(4):
+            self.back_y(k, d).wait_recv()
         self.kept(k).start()
-        for copy in (self.over_core, self.over_x, self.over_y, self.back_y):
-            copy(k).wait_send()
+        self.over_core(k).wait_send()
+        for h in range(2):
+            self.over_x(k, h).wait_send()
+        for d in range(4):
+            self.over_y(k, d).wait_send()
+            self.back_y(k, d).wait_send()
         for d in range(1, 4):
             self.over_z(k, d).wait_send()
             self.back_z(k, d).wait_send()
@@ -422,46 +440,39 @@
     return (w.astype(F32) - 0.02 * step).astype(BF), m, v
 
 
-def columns_kernel(early, late, *refs):
+def update_kernel(early, late, early_rows, late_rows, *refs):
+    *refs, turned = refs
     rows = refs[0].shape[1]
     part = early.shape[-1]
-
-    def take(chunks):
-        for chunk, (g, n) in enumerate(chunks):
+    layer, s = pl.program_id(0), pl.program_id(1)
+    skip = 2 * rows - early.shape[3]
+
+    def take(columns, downs):
+        for chunk, (g, n) in enumerate(columns):
             at = slice(chunk * part, (chunk + 1) * part)
-            both = jnp.concatenate([g[n, 0, 0], g[n, 1, 0, : 2 * rows - g.shape[3]]], 0)
+            both = jnp.concatenate([g[n, 0, 0], g[n, 1, 0, :skip]], 0)
             for i in range(2):
-                w, m, v = (refs[3 * i + k][0, :, at] for k in range(3))
-                new = adamw(w, m, v, both[i * rows : (i + 1) * rows])
+                new = adamw(*(refs[3 * i + k][0, :, at] for k in range(3)), both[i * rows : (i + 1) * rows])
                 for k in range(3):
-                    refs[6 + 3 * i + k][0, :, at] = new[k]
-
-    @pl.when(pl.program_id(0) == 0)
-    def _():
-        take([(late, CHUNKS - EARLY + n) for n in range(CHUNKS)])
-
-    @pl.when(pl.program_id(0) == 1)
-    def _():
-        take([(early, n) for n in range(EARLY)] + [(late, n) for n in range(CHUNKS - EARLY)])
-
-
-def rows_kernel(early, late, w, m, v, *outs):
-    def take(g):
-        rows = w.shape[2] // 4
-        skip = g.shape[3] - rows
-        turned = jnp.concatenate([g[0, 0, q, skip:] for q in range(4)], 0).T
-        for out, new in zip(outs, adamw(w[0], m[0], v[0], turned), strict=True):
-            out[0] = new
-
-    from_early = (pl.program_id(0) == 1) & (pl.program_id(1) < EARLY)
-
-    @pl.when(from_early)
-    def _():
-        take(early)
-
-    @pl.when(jnp.logical_not(from_early))
-    def _():
-        take(late)
+                    refs[9 + 3 * i + k][0, :, at] = new[k]
+
+        @pl.when(s == 0)
+        def _():
+            for chunk, (g, n) in enumerate(downs):
+                turned[chunk * part : (chunk + 1) * part, :] = jnp.concatenate([g[n, 0, q, skip:] for q in range(4)], 0).T
+
+    def chunks(low, high):
+        return [(high, CHUNKS - EARLY + n) for n in range(CHUNKS)], [(low, n) for n in range(EARLY)] + [(high, n) for n in range(CHUNKS - EARLY)]
+
+    for number in range(2):
+
+        @pl.when(layer == number)
+        def _(number=number):
+            take(chunks(early, late)[number], chunks(early_rows, late_rows)[number])
+
+    new = adamw(*(refs[6 + k][0] for k in range(3)), turned[pl.ds(pl.multiple_of(s * rows, rows), rows), :])
+    for k in range(3):
+        refs[15 + k][0] = new[k]
 
 
 def solution(mesh):
@@ -528,30 +539,20 @@
 
         g = [total.reshape(-1, 2, 4, deep // 2, part) for total in (early, rest)]
         block = pl.BlockSpec((1, rows, CHUNKS * part), lambda layer, s: (layer, 0, s))
-        both = [pl.BlockSpec((total.shape[0], 2, 1, deep // 2, part), lambda layer, s: (0, 0, s, 0, 0)) for total in g]
+        quarter = pl.BlockSpec((1, rows, d), lambda layer, s: (layer, s, 0))
+        columns = [pl.BlockSpec((total.shape[0], 2, 1, deep // 2, part), lambda layer, s: (0, 0, s, 0, 0)) for total in g]
+        downs = [pl.BlockSpec((total.shape[0], 1, 4, deep // 2, part), lambda layer, s: (0, 1, 0, 0, 0)) for total in g]
+        blocks = [block] * 6 + [quarter] * 3
         new = pl.pallas_call(
-            columns_kernel,
+            update_kernel,
             grid=(layers, 4),
-            in_specs=both + [block] * 6,
-            out_specs=[block] * 6,
-            out_shape=[shape((layers, rows, ff), t) for t in (BF, F32, F32)] * 2,
-            name="columns",
+            in_specs=columns + downs + blocks,
+            out_specs=blocks,
+            out_shape=[shape(weights[i].shape, t) for i in range(3) for t in (BF, F32, F32)],
+            scratch_shapes=[pltpu.VMEM((CHUNKS * part, d), BF)],
+            name="update",
             **params(1),
-        )(*g, weights[0], m[0], v[0], weights[1], m[1], v[1])
-        block = pl.BlockSpec((1, part, d), lambda layer, j: (layer, j, 0))
-        both = [
-            pl.BlockSpec((1, 1, 4, deep // 2, part), lambda layer, j: (jnp.minimum(j, EARLY - 1), 1, 0, 0, 0)),
-            pl.BlockSpec((1, 1, 4, deep // 2, part), lambda layer, j: (jnp.where(layer == 0, j + CHUNKS - EARLY, jnp.maximum(j - EARLY, 0)), 1, 0, 0, 0)),
-        ]
-        new += pl.pallas_call(
-            rows_kernel,
-            grid=(layers, CHUNKS),
-            in_specs=both + [block] * 3,
-            out_specs=[block] * 3,
-            out_shape=[shape((layers, CHUNKS * part, d), t) for t in (BF, F32, F32)],
-            name="rows",
-            **params(1),
-        )(*g, weights[2], m[2], v[2])
+        )(*g, *g, *(one for i in range(3) for one in (weights[i], m[i], v[i])))
         return tuple(new[3 * i + k] for k in range(3) for i in range(3))
 
     states, cut = P(("rep", "r", "s"), None, None), P(None, "s", None)

time: 427 us -> 412 us (0.965)
  Pallas kernels: 425 us -> 412 us
    pallas_call x1, Pallas kernels: 146 us -> 137 us  [step(): pl.pallas_call(functools.partial(backward_kernel, True), grid=(CHUNKS, ST...]
    pallas_call x2 -> x1, Pallas kernels: 27.6 us -> 22.3 us  [step(): pl.pallas_call(update_kernel, grid=(layers, 4), in_specs=columns + downs...]
where the time goes in v3:
time: 412 us
  Pallas kernels  412 us (100%)
    pallas_call x1, Pallas kernels, step(): pl.pallas_call(functools.partial(backward_kernel, False), grid=(CHUNKS, S...  163 us
    pallas_call x1, Pallas kernels, step(): pl.pallas_call(functools.partial(backward_kernel, True), grid=(CHUNKS, ST...  137 us
    pallas_call x1, Pallas kernels, step(): pl.pallas_call(forward_kernel, grid=(CHUNKS, STEPS), in_specs=[pl.BlockSp...  90 us
    pallas_call x1, Pallas kernels, step(): pl.pallas_call(update_kernel, grid=(layers, 4), in_specs=columns + downs...  22.3 us

profile of v3, /device:TPU:0, one launch (start us, length us, event | category | flops | bytes accessed | tf_op | source)
XLA Modules:
  0.0 412.3 jit_solution(7325500702311273811)
XLA Ops:
  0.6 90.0 %forward.1 = (bf16[10,2,2,480,512]{4,3,2,1,0:T(8,128)(2,1)}, bf16[4096,640]{1,0:T(8,128)(2,1)}, f32[5,4096,512]{2,1,0:T(8,128)}, f32[5,4096,512]{2,1,0:T(8,128)}) custom-call(bf16[2,160,2560]{2,1,0:T(8,128)(2,1)} %refs_0_.1, bf16[2,160,2560]{2,1,0:T(8,128)(2,1)} %refs_3_.1, bf16[2,640,640]{2,1,0:T(8,128)(2,1)} %refs_6_.1, bf16[4096,640]{1,0:T(8,128)(2,1)} %bitcast.9), custom_call_target="tpu_custom_call" | custom-call | flops 40265318400 | tf_op jit(solution)/shard_map/forward/pallas_call | solution.py:506
  90.6 162.6 %backward_1.1 = (bf16[3,8,240,128]{3,2,1,0:T(8,128)(2,1)}, bf16[2,2,2,480,512]{4,3,2,1,0:T(8,128)(2,1)}, bf16[4096,640]{1,0:T(8,128)(2,1)}) custom-call(bf16[4096,640]{1,0:T(8,128)(2,1)} %get-tuple-element.25.h_ref, bf16[4096,640]{1,0:T(8,128)(2,1)} %bitcast.8, bf16[10,2,2,480,512]{4,3,2,1,0:T(8,128)(2,1)} %get-tuple-element.26.w_ref), custom_call_target="tpu_custom_call" | custom-call | flops 107374182400 | tf_op jit(solution)/shard_map/backward_1/pallas_call | solution.py:519
  253.2 136.7 %backward_0.1 = bf16[7,8,240,128]{3,2,1,0:T(8,128)(2,1)} custom-call(bf16[4096,640]{1,0:T(8,128)(2,1)} %bitcast.10, bf16[4096,640]{1,0:T(8,128)(2,1)} %get-tuple-element.28.dy_ref, bf16[10,2,2,480,512]{4,3,2,1,0:T(8,128)(2,1)} %get-tuple-element.26.w_ref, f32[5,4096,512]{2,1,0:T(8,128)} %get-tuple-element.29.refs_0_, ...), custom_call_target="tpu_custom_call" | custom-call | flops 53687091200 | tf_op jit(solution)/shard_map/backward_0/pallas_call | solution.py:529
  389.9 22.3 %update.1 = (bf16[2,160,2560]{2,1,0:T(8,128)(2,1)}, f32[2,160,2560]{2,1,0:T(8,128)}, f32[2,160,2560]{2,1,0:T(8,128)}, bf16[2,160,2560]{2,1,0:T(8,128)(2,1)}, f32...) custom-call(bf16[3,2,4,240,128]{4,3,2,1,0:T(8,128)(2,1)} %bitcast.6,, ...), custom_call_target="tpu_custom_call" | custom-call | flops 6710886400 | tf_op jit(solution)/shard_map/update/pallas_call | solution.py:546
